TPU v7x, 32 devices: a whole 2x2x4 slice. The times are simulated.
32 devices in a mesh: rows: 8 (over z, y), par: 4 (over x, core).
Axes of the slice: x: 2, y: 2, z: 4, core: 2. Of those that a mesh axis runs over, the one named last changes fastest.
Arguments:
- base_a: bfloat16 [4, 64, 256], P(None, 'rows'), may hold values from -6 to 6
- base_b: bfloat16 [4, 64, 256], P(None, 'rows'), may hold values from -6 to 6
- input_scale: float32 [256], replicated, may hold values from 0.1 to 3
- layer_one: bfloat16 [256, 1024], replicated, may hold values from -0.375 to 0.375
- layer_two: bfloat16 [1024, 1024], replicated, may hold values from -0.1875 to 0.1875
- layer_three: bfloat16 [1024, 128], replicated, may hold values from -0.1875 to 0.1875
- swap_cols: int32 [256], P('par'), may hold values from 0 to 255, each once
- window_ends: int32 [4], replicated, may hold values from 32 to 64
Outputs:
- first_order: float32 [4, 256, 128], P(None, 'par')
- total_order: float32 [4, 256, 128], P(None, 'par')
- total_variance: float32 [4, 128], replicated
Inputs may be any that keep to these rules, and one draw needn't show every extreme that they name: window w uses its rows 0 to window_ends[w] - 1. `swap_cols`: each column appears once.
All inputs are finite; a program needn't handle non-finite values.
Results may differ from a plain program's by a relative error of at most 0.0055.
The roundings to bfloat16 on the way count: a program that leaves them out, or rounds other values in their place, can miss the bound.
Values sent between devices are 32-bit elements; how exact they have to be, the bound alone decides.
No kernel may reach another device: no remote copies, remote signals or barrier semaphores. Data moves between devices by JAX's collectives and lax.ppermute only.
A program may use at most 64 MiB of HBM per device.

v0:
```python
import jax
import jax.numpy as jnp
from jax import lax
from jax.sharding import PartitionSpec as P


def network_tail(first_pre, layer_two, layer_three):
    hidden_one = jax.nn.silu(first_pre).astype(jnp.bfloat16)
    second_pre = jnp.dot(hidden_one, layer_two, preferred_element_type=jnp.float32)
    hidden_two = jax.nn.silu(second_pre).astype(jnp.bfloat16)
    return jnp.dot(hidden_two, layer_three, preferred_element_type=jnp.float32)


def merge_total(former, latter):
    counts = former[0] + latter[0]
    inverse = 1.0 / jnp.maximum(counts, 1.0)
    change = latter[1] - former[1]
    return (
        counts,
        former[1] + change * latter[0] * inverse,
        former[2] + latter[2] + change * change * former[0] * latter[0] * inverse,
    )


def merge_groups(former, latter):
    counts = former[0] + latter[0]
    inverse = 1.0 / jnp.maximum(counts, 1.0)
    change_b = latter[1] - former[1]
    change_d = latter[2] - former[2]
    pair_weight = former[0] * latter[0] * inverse
    return (
        counts,
        former[1] + change_b * latter[0] * inverse,
        former[2] + change_d * latter[0] * inverse,
        former[3] + latter[3] + change_d * change_d * pair_weight,
        former[4] + latter[4] + change_b * change_d * pair_weight,
    )


def pick_window(states, window):
    return tuple((member[window : window + 1] for member in states))


def join_windows(*pieces):
    return jnp.concatenate(pieces, 0)


def conclude_states(total_state, group_state, windows):
    firsts = []
    totals = []
    variances = []
    running_total = None
    running_groups = None
    for window in range(windows):
        total_now = tuple((member[window] for member in total_state))
        group_now = tuple((member[window] for member in group_state))
        if window == 0:
            running_total = total_now
            running_groups = group_now
        else:
            running_total = merge_total(running_total, total_now)
            running_groups = merge_groups(running_groups, group_now)
        variance = running_total[2] / running_total[0]
        firsts.append(running_groups[4] / running_groups[0] / variance)
        totals.append(
            0.5
            * (running_groups[3] / running_groups[0] + running_groups[2] * running_groups[2])
            / variance
        )
        variances.append(variance)
    return (jnp.stack(firsts), jnp.stack(totals), jnp.stack(variances))


def local(base_a, base_b, input_scale, layer_one, layer_two, layer_three, swap_cols, window_ends):
    windows, window_rows, width = base_a.shape
    par_size = lax.axis_size("par")
    quarter = window_rows // par_size
    groups = swap_cols.shape[0]
    hidden = layer_one.shape[1]
    outputs = layer_three.shape[1]
    all_rows = windows * window_rows
    row_start = lax.axis_index("rows") * window_rows
    usable = (
        row_start + jnp.arange(window_rows, dtype=jnp.int32)[None, :] < window_ends[:, None]
    ).astype(jnp.float32)
    inputs_a = (base_a.astype(jnp.float32) * input_scale).astype(jnp.bfloat16)
    inputs_b = (base_b.astype(jnp.float32) * input_scale).astype(jnp.bfloat16)
    flat_a = inputs_a.reshape(all_rows, width)
    flat_b = inputs_b.reshape(all_rows, width)
    preact_a = jnp.dot(flat_a, layer_one, preferred_element_type=jnp.float32)
    offset = lax.axis_index("par") * quarter
    quarter_a = lax.dynamic_slice_in_dim(
        preact_a.reshape(windows, window_rows, hidden), offset, quarter, 1
    )
    quarter_inputs_b = lax.dynamic_slice_in_dim(inputs_b, offset, quarter, 1).reshape(
        windows * quarter, width
    )
    quarter_b = jnp.dot(quarter_inputs_b, layer_one, preferred_element_type=jnp.float32)
    quarter_pre = jnp.concatenate([quarter_a.reshape(windows * quarter, hidden), quarter_b], 0)
    quarter_out = network_tail(quarter_pre, layer_two, layer_three).reshape(
        2, windows, quarter, outputs
    )
    out_a_part = quarter_out[0]
    out_b_part = quarter_out[1]
    usable_part = lax.dynamic_slice_in_dim(usable, offset, quarter, 1)
    out_a, out_b = (
        lax.all_gather(out_a_part, "par", axis=1, tiled=True),
        lax.all_gather(out_b_part, "par", axis=1, tiled=True),
    )
    chosen_a = jnp.take(flat_a, swap_cols, axis=1).astype(jnp.float32)
    chosen_b = jnp.take(flat_b, swap_cols, axis=1).astype(jnp.float32)
    chosen_rows = jnp.take(layer_one, swap_cols, axis=0).astype(jnp.float32)
    preact_c = (
        preact_a[None, :, :]
        + jnp.transpose(chosen_b - chosen_a)[:, :, None] * chosen_rows[:, None, :]
    )
    out_c = network_tail(preact_c.reshape(groups * all_rows, hidden), layer_two, layer_three)
    differ = out_c.reshape(groups, windows, window_rows, outputs) - out_a[None]
    mask_rows = usable[:, :, None]
    mask_part = usable_part[:, :, None]
    pooled_sum = jnp.sum(mask_part * (out_a_part + out_b_part), axis=1)
    pooled_squares = jnp.sum(
        mask_part * (out_a_part * out_a_part + out_b_part * out_b_part), axis=1
    )
    total_part = (pooled_sum, pooled_squares)
    masked_d = differ * mask_rows[None]
    sum_b = jnp.sum(mask_rows * out_b, axis=1)[:, None, :]
    sum_d = jnp.transpose(jnp.sum(masked_d, axis=2), (1, 0, 2))
    squares_d = jnp.transpose(jnp.sum(masked_d * differ, axis=2), (1, 0, 2))
    cross_raw = jnp.transpose(jnp.sum(masked_d * out_b[None], axis=2), (1, 0, 2))
    group_part = (sum_b, sum_d, squares_d, cross_raw)

    def settle(total_piece, group_piece, ends_piece):
        total_sum, total_squares = lax.psum(total_piece, ("rows", "par"))
        group_b, group_d, group_squares, group_cross = lax.psum(group_piece, "rows")
        counts = ends_piece.astype(jnp.float32)[:, None, None]
        pooled_counts = 2.0 * counts[:, :, 0]
        total_mean = total_sum / pooled_counts
        total_state = (pooled_counts, total_mean, total_squares - total_sum * total_mean)
        mean_b = group_b / counts
        mean_d = group_d / counts
        group_state = (
            counts,
            mean_b,
            mean_d,
            group_squares - group_d * mean_d,
            group_cross - group_b * mean_d,
        )
        return (total_state, group_state)

    per_window = [
        settle(
            pick_window(total_part, window),
            pick_window(group_part, window),
            window_ends[window : window + 1],
        )
        for window in range(windows)
    ]
    settled = jax.tree.map(join_windows, *per_window)
    return conclude_states(settled[0], settled[1], windows)


def solution(mesh):
    in_specs = (P(None, "rows", None), P(None, "rows", None), P(), P(), P(), P(), P("par"), P())
    out_specs = (P(None, "par", None), P(None, "par", None), P())
    return jax.shard_map(local, mesh=mesh, in_specs=in_specs, out_specs=out_specs, check_vma=False)
```

profile of v0, /device:TPU:0, one launch (start us, length us, event | category | flops | bytes accessed | tf_op | source)
XLA Modules:
  0.0 131.8 jit_solution(2429451299486696578)
XLA Ops:
  7.2 0.0 copy-start
  7.2 0.0 all-reduce.4.cloned.1.call-start
  7.2 0.8 compare_and_fusion
  8.0 0.7 compare_select_fusion
  8.7 0.7 compare_convert_fusion
  9.4 0.1 copy.29
  9.5 0.8 fusion.14
  10.3 0.1 copy.26
  10.4 1.2 fusion.29
  11.6 1.2 fusion.31
  12.9 0.0 copy-done
  12.9 1.5 %fusion.11 = f32[16,128]{1,0:T(8,128)S(1)} fusion(bf16[1024,128]{1,0:T(8,128)(2,1)} %param.15, bf16[1024,1024]{1,0:T(8,128)(2,1)S(1)} %copy-done, f32[8,1024]{1,0:T(8,128)S(1)} %fusion.31, f32[8,1024]{1,0:T(8,128)S(1)} %reshape.400), kind=kOutput, calls=%fused_computation.28 | convolution fusion | flops 37928960 | bytes 2433024 | tf_op jit(solution)/shard_map/dot_general | solution.py:11
  14.4 6.2 %all_gather.7 = f32[4,8,128]{2,0,1:T(4,128)S(1)} all-gather(f32[4,2,128]{2,0,1:T(4,128)S(1)} %copy.30), channel_id=1, replica_groups=mesh['rows'=8,'par'=4] {'par'}, dimensions={1}, use_global_device_ids=true | all-gather | bytes 20480 | tf_op jit(solution)/shard_map/all_gather | solution.py:108
  20.7 0.1 multiply_reduce_fusion.1
  20.8 0.1 copy.25
  20.9 1.9 %gather_fusion = bf16[64,1024]{1,0:T(8,128)(2,1)S(1)} fusion(bf16[256,1024]{1,0:T(8,128)(2,1)} %param.13, s32[1024]{0:T(1024)S(1)} %pad_clamp_fusion), kind=kCustom, calls=%fused_computation.2 | custom fusion | bytes 262400 | tf_op jit(solution)/shard_map/jit(_take)/gather | solution.py:112
  22.8 0.6 gather_fusion.1
  23.4 0.6 gather_fusion.2
  24.1 0.1 subtract_bitcast_fusion
  24.2 0.1 mul.598
  24.2 0.6 slice_bitcast_fusion
  24.8 5.4 %all_gather.6 = f32[4,8,128]{2,0,1:T(4,128)S(1)} all-gather(f32[4,2,128]{2,0,1:T(4,128)S(1)} %copy.27), channel_id=1, replica_groups=mesh['rows'=8,'par'=4] {'par'}, dimensions={1}, use_global_device_ids=true | all-gather | bytes 20480 | tf_op jit(solution)/shard_map/all_gather | solution.py:107
  30.2 0.1 select_convert_fusion
  30.3 2.4 %fusion.6 = bf16[2048,1024]{1,0:T(8,128)(2,1)S(1)} fusion(f32[64,1024]{1,0:T(8,128)S(1)} %select_convert_fusion, f32[2048]{0:T(1024)S(1)} %mul.598, f32[32,1024]{1,0:T(8,128)S(1)} %fusion.29), kind=kLoop, calls=%fused_computation.10 | loop fusion | flops 14680064 | bytes 4595712 | tf_op jit(solution)/shard_map/convert_element_type | solution.py:8
  32.7 0.0 copy-start.1
  32.7 4.5 %fusion.30 = f32[2048,1024]{1,0:T(8,128)S(1)} fusion(bf16[2048,1024]{1,0:T(8,128)(2,1)S(1)} %fusion.6, bf16[1024,1024]{1,0:T(8,128)(2,1)S(1)} %copy-done), kind=kOutput, calls=%fused_computation.102 | convolution fusion | flops 4294967296 | bytes 14680064 | tf_op jit(solution)/shard_map/dot_general | solution.py:9
  37.3 0.0 copy-done.1
  37.3 0.0 copy-start.2
  37.3 3.0 %fusion.9 = (f32[64,4,128]{2,1,0:T(4,128)S(1)}, f32[64,4,128]{2,1,0:T(4,128)S(1)}, f32[64,4,128]{2,1,0:T(4,128)S(1)}) fusion(f32[4,8]{1,0:T(4,128)S(1)} %copy.29, f32[4,8,128]{2,1,0:T(8,128)S(1)} %copy.28, f32[4,8,128]{2,1,0:T(8,128)S(1)} %copy.31, bf16[1024,128]{1,0:T(8,128)(2,1)S(1)} %copy-done.1, f32[2048,1024]{1,0:T(8,128)S(1)} %fusion.30), kind=kOutput, calls=%fused_computation.17 | convolution fusion | flops 549093376 | bytes 9076864 | tf_op jit(solution)/shard_map/dot_general | solution.py:11
  40.4 0.7 fusion.22
  41.0 0.6 fusion.24
  41.7 0.7 fusion.23
  42.4 0.0 all-reduce.4.cloned.1.call-update
  42.4 0.0 copy-done.2
  42.4 0.6 fusion.28
  44.9 0.1 copy.34
  45.0 0.1 multiply_reduce_fusion.2
  45.1 40.8 %all-reduce = (f32[1,128]{1,0:T(1,128)S(1)}, f32[1,128]{1,0:T(1,128)S(1)}, f32[1,128]{1,0:T(1,128)S(1)}, f32[1,128]{1,0:T(1,128)S(1)}, f32[1,128]{1,0:T(1,128)S(...) all-reduce(f32[1,128]{1,0:T(1,128)S(1)} %get-tuple-element.105, ...), channel_id=1, replica_groups=mesh['rows'=8,'par'=4] {'rows','par'}, use_global_device_ids=true, to_apply=%region_13.15 | all-reduce | flops 1024 | bytes 8192 | tf_op jit(solution)/shard_map/psum | solution.py:134
  86.8 0.6 pad_maximum_fusion.3
  87.4 32.3 %all-reduce.4.cloned.1.call-done = (f32[1,64,128]{2,1,0:T(8,128)}, f32[1,1,128]{2,1,0:T(1,128)}, f32[1,1,128]{2,1,0:T(1,128)}, f32[1,64,128]{2,1,0:T(8,128)}, f3...) async-done(((f32[1,64,128]{2,1,0:T(8,128)}, ...) | async-done | bytes 395280 | tf_op jit(solution)/shard_map/psum | solution.py:135
  119.7 0.7 bitcast_add_fusion
  120.4 0.6 bitcast_subtract_fusion
  121.0 0.9 broadcast_divide_fusion.2
  121.9 0.8 multiply_divide_fusion.1
  122.8 0.8 multiply_divide_fusion
  123.6 0.7 pad_maximum_fusion.1
  124.3 0.7 pad_maximum_fusion
  (18 shorter events, 0.2 us)
Async XLA Ops:
  7.2 5.8 %copy-start = (bf16[1024,1024]{1,0:T(8,128)(2,1)S(1)}, bf16[1024,1024]{1,0:T(8,128)(2,1)}, u32[]{:S(2)}) copy-start(bf16[1024,1024]{1,0:T(8,128)(2,1)} %param.14) | copy-start | bytes 6291460
  7.2 112.5 %all-reduce.4.cloned.1.call-start = ((), (), s32[]{:S(2)}) async-start(), calls=%async_computation | async-start | bytes 790528 | tf_op jit(solution)/shard_map/psum | solution.py:135
  32.7 4.5 %copy-start.1 = (bf16[1024,128]{1,0:T(8,128)(2,1)S(1)}, bf16[1024,128]{1,0:T(8,128)(2,1)}, u32[]{:S(2)}) copy-start(bf16[1024,128]{1,0:T(8,128)(2,1)} %param.15) | copy-start | bytes 786436
  37.3 5.1 %copy-start.2 = (s32[4]{0:T(128)S(1)}, s32[4]{0:T(128)}, u32[]{:S(2)}) copy-start(s32[4]{0:T(128)} %param.17) | copy-start | bytes 52
Sparse Core Ops, SparseCore 0:
  42.5 77.1 all-reduce.3
where the time goes:
time: 133 us; the launch traced here: 132 us
  blocking collectives  52.4 us (39%)
  waiting for transfers between devices  32.3 us (24%)
  between operations  16.9 us (13%)
  other arithmetic  11.5 us (9%)
  matrix products  11.5 us (9%)
  local copies, waits for them, and re-layouts  7.03 us (5%)
    psum x1, blocking collectives, settle(): total_sum, total_squares = lax.psum(total_piece, ('rows', 'par'))  40.8 us
    psum x1, waiting for transfers between devices, settle(): group_b, group_d, group_squares, group_cross = lax.psum(group_piece, 'rows')  32.3 us
    all_gather x1, blocking collectives, local(): lax.all_gather(out_b_part, 'par', axis=1, tiled=True)  6.23 us
    all_gather x1, blocking collectives, local(): lax.all_gather(out_a_part, 'par', axis=1, tiled=True)  5.42 us
    dot_general x1, matrix products, network_tail(): jnp.dot(hidden_one, layer_two, preferred_element_type=jnp.float32)  4.53 us
    dot_general x2, matrix products, network_tail(): return jnp.dot(hidden_two, layer_three, preferred_element_type=jnp.float32)  4.52 us
  transfers between devices with their start and end apart: 1, of which 1 were waited for; matrix products, arithmetic and copies ran while one was open for 1% of the time, Pallas kernels for 0%

commit v1 on v0

v1 whole, which is shorter than its diff:
```python
import math

import jax
import jax.numpy as jnp
from jax import lax
from jax.experimental import pallas as pl
from jax.experimental.pallas import tpu as pltpu
from jax.sharding import PartitionSpec as P

CHUNK_ROWS = 512
COLUMN_TILE = 256


def dot(left, right):
    return jnp.dot(left, right, preferred_element_type=jnp.float32)


def silu_half(half):
    return half + half * jnp.tanh(half)


def evaluate_kernel(
    front,
    back,
    own_ref,
    *refs,
):
    peers = refs[: front - 1]
    (scale_ref, one_hbm, two_hbm, three_hbm, cols_ref, ends_ref, out_ref) = refs[front - 1 : front + 6]
    (one_ref, two_ref, three_ref, pre_ref, first_ref, second_ref, result_ref, base_ref, sems) = refs[front + 6 :]
    windows, block_rows, width = own_ref.shape[1:]
    hidden = one_ref.shape[1]
    outputs = three_ref.shape[1]
    total_groups = cols_ref.shape[0]
    groups = total_groups // front
    rows = front * windows * block_rows
    copies = [
        pltpu.make_async_copy(source, target, sems.at[index])
        for index, (source, target) in enumerate(
            ((one_hbm, one_ref), (two_hbm, two_ref), (three_hbm, three_ref))
        )
    ]
    for copy in copies:
        copy.start()
    device = lax.axis_index("rows")
    place = device // back
    corner = device % back
    scale = scale_ref[...]
    pieces = [own_ref] + list(peers)

    def scaled(which):
        return jnp.concatenate(
            [(piece[which].reshape(windows * block_rows, width) * scale).astype(jnp.bfloat16) for piece in pieces], 0
        )

    inputs_a = scaled(0)
    inputs_b = scaled(1)
    row_ids = lax.broadcasted_iota(jnp.int32, (groups, width), 0)
    lane_ids = lax.broadcasted_iota(jnp.int32, (groups, width), 1)
    wanted = jnp.zeros((groups, width), jnp.int32)
    for group in range(groups):
        wanted = jnp.where(row_ids == group, cols_ref[place * groups + group], wanted)
    picks = jnp.where(lane_ids == wanted, 1.0, 0.0).astype(jnp.bfloat16)
    contract = (((1,), (1,)), ((), ()))
    delta = 0.5 * (
        lax.dot_general(inputs_b, picks, contract, preferred_element_type=jnp.float32)
        - lax.dot_general(inputs_a, picks, contract, preferred_element_type=jnp.float32)
    )
    copies[0].wait()
    picked = dot(picks, one_ref[...])
    inputs_ab = jnp.concatenate([inputs_a, inputs_b], 0)
    for start in range(0, hidden, COLUMN_TILE):
        tile = slice(start, start + COLUMN_TILE)
        half = 0.5 * dot(inputs_ab, one_ref[:, tile])
        pre_ref[:, tile] = half[:rows]
        first_ref[0, : 2 * rows, tile] = silu_half(half).astype(jnp.bfloat16)
    copies[1].wait()
    copies[2].wait()

    def tail(slot, size):
        for start in range(0, hidden, COLUMN_TILE):
            tile = slice(start, start + COLUMN_TILE)
            half = 0.5 * dot(first_ref[slot, :size], two_ref[:, tile])
            second_ref[slot, :size, tile] = silu_half(half).astype(jnp.bfloat16)
        return dot(second_ref[slot, :size], three_ref[...])

    base_ref[...] = tail(0, 2 * rows)
    out_a = base_ref[:rows]
    out_b = base_ref[rows:]
    sublane = lax.broadcasted_iota(jnp.int32, (block_rows, outputs), 0)
    masks = []
    for peer in range(front):
        member = jnp.bitwise_xor(place, peer) if front & (front - 1) == 0 else lax.rem(place + peer, front)
        first_row = (member * back + corner) * block_rows
        masks.append([jnp.where(sublane + first_row < ends_ref[w], 1.0, 0.0) for w in range(windows)])

    def block(values, peer, window):
        at = (peer * windows + window) * block_rows
        return values[at : at + block_rows]

    for window in range(windows):
        sums = [jnp.zeros((block_rows, outputs), jnp.float32) for _ in range(3)]
        for peer in range(front):
            mask = masks[peer][window]
            va = block(out_a, peer, window)
            vb = block(out_b, peer, window)
            sums[0] += mask * vb
            sums[1] += mask * (va + vb)
            sums[2] += mask * (va * va + vb * vb)
        lines = [jnp.sum(value, axis=0, keepdims=True) for value in sums]
        lines.append(jnp.zeros((8 - len(lines), outputs), jnp.float32))
        out_ref[window, 3 * groups :, :] = jnp.concatenate(lines, 0)

    per_chunk = max(1, min(groups, CHUNK_ROWS // rows))

    def fill(chunk, slot):
        for index in range(per_chunk):
            group = chunk * per_chunk + index
            change = delta[:, group : group + 1]
            for start in range(0, hidden, COLUMN_TILE):
                tile = slice(start, start + COLUMN_TILE)
                half = pre_ref[:, tile] + change * picked[group : group + 1, tile]
                first_ref[slot, index * rows : (index + 1) * rows, tile] = silu_half(half).astype(jnp.bfloat16)

    chunks = groups // per_chunk
    fill(0, 1)
    for chunk in range(chunks):
        slot = (chunk + 1) % 2
        if chunk + 1 < chunks:
            fill(chunk + 1, 1 - slot)
        values = tail(slot, per_chunk * rows)
        for index in range(per_chunk):
            group = chunk * per_chunk + index
            for window in range(windows):
                sums = [jnp.zeros((block_rows, outputs), jnp.float32) for _ in range(3)]
                for peer in range(front):
                    at = index * rows + (peer * windows + window) * block_rows
                    differ = values[at : at + block_rows] - block(base_ref, peer, window)
                    masked = masks[peer][window] * differ
                    sums[0] += masked
                    sums[1] += masked * differ
                    sums[2] += masked * base_ref[pl.ds(rows + (peer * windows + window) * block_rows, block_rows)]
                for kind in range(3):
                    out_ref[window, kind * groups + group : kind * groups + group + 1, :] = jnp.sum(
                        sums[kind], axis=0, keepdims=True
                    )


def conclude_kernel(groups, own_ref, other_ref, ends_ref, out_ref, variance_ref):
    windows = own_ref.shape[0]
    running = jnp.zeros(own_ref.shape[1:], jnp.float32)
    count = jnp.int32(0)
    for window in range(windows):
        running = running + (own_ref[window] + other_ref[window])
        count = count + ends_ref[window]
        share = 1.0 / (jnp.zeros((1, own_ref.shape[2]), jnp.float32) + count.astype(jnp.float32))
        sum_b = running[3 * groups : 3 * groups + 1]
        sum_all = running[3 * groups + 1 : 3 * groups + 2]
        squares = running[3 * groups + 2 : 3 * groups + 3]
        mean = sum_all * (0.5 * share)
        variance = (squares - sum_all * mean) * (0.5 * share)
        mean_d = running[:groups] * share
        weight = share / variance
        out_ref[0, window] = (running[2 * groups : 3 * groups] - sum_b * mean_d) * weight
        out_ref[1, window] = running[groups : 2 * groups] * (0.5 * weight)
        variance_ref[window : window + 1, :] = variance


def assemble_kernel(front, back, own_ref, *refs):
    peers = refs[: front - 1]
    first_ref, total_ref = refs[front - 1 :]
    place = lax.axis_index("rows") // back
    groups = own_ref.shape[2]
    for peer, ref in enumerate([own_ref] + list(peers)):
        member = jnp.bitwise_xor(place, peer) if front & (front - 1) == 0 else lax.rem(place + peer, front)
        start = pl.multiple_of(member * groups, groups)
        first_ref[:, pl.ds(start, groups), :] = ref[0]
        total_ref[:, pl.ds(start, groups), :] = ref[1]


def swap_with(values, pairs):
    return lax.ppermute(values, "rows", pairs)


def local(base_a, base_b, input_scale, layer_one, layer_two, layer_three, swap_cols, window_ends):
    windows, block_rows, width = base_a.shape
    size = lax.axis_size("rows")
    total_groups = swap_cols.shape[0]
    hidden = layer_one.shape[1]
    outputs = layer_three.shape[1]
    back = 2 if size % 2 == 0 else 1
    front = size // back
    groups = total_groups // front
    rows = front * windows * block_rows

    def pairs_of(peer):
        pairs = []
        for device in range(size):
            place, corner = divmod(device, back)
            source = (place ^ peer) if front & (front - 1) == 0 else (place + peer) % front
            pairs.append((source * back + corner, device))
        return pairs

    own = jnp.stack([base_a, base_b]).astype(jnp.float32)
    received = [swap_with(own, pairs_of(peer)) for peer in range(1, front)]
    vmem = pl.BlockSpec(memory_space=pltpu.VMEM)
    smem = pl.BlockSpec(memory_space=pltpu.SMEM)
    anywhere = pl.BlockSpec(memory_space=pl.ANY)
    per_chunk = max(1, min(groups, CHUNK_ROWS // rows))
    room = max(2, per_chunk) * rows
    height = 3 * groups + 8

    def evaluate(*args):
        return evaluate_kernel(front, back, *args)

    partial = pl.pallas_call(
        evaluate,
        out_shape=jax.ShapeDtypeStruct((windows, height, outputs), jnp.float32),
        in_specs=[vmem] * (front + 1) + [anywhere] * 3 + [smem] * 2,
        out_specs=vmem,
        scratch_shapes=[
            pltpu.VMEM(layer_one.shape, jnp.bfloat16),
            pltpu.VMEM(layer_two.shape, jnp.bfloat16),
            pltpu.VMEM(layer_three.shape, jnp.bfloat16),
            pltpu.VMEM((rows, hidden), jnp.float32),
            pltpu.VMEM((2, room, hidden), jnp.bfloat16),
            pltpu.VMEM((2, room, hidden), jnp.bfloat16),
            pltpu.VMEM((room, outputs), jnp.float32),
            pltpu.VMEM((2 * rows, outputs), jnp.float32),
            pltpu.SemaphoreType.DMA((3,)),
        ],
        name="evaluate",
    )(own, *received, input_scale.reshape(1, width), layer_one, layer_two, layer_three, swap_cols, window_ends)

    if back == 2:
        other = swap_with(partial, [(device, device ^ 1) for device in range(size)])
    else:
        other = jnp.zeros_like(partial)

    def conclude(*args):
        return conclude_kernel(groups, *args)

    settled, variance = pl.pallas_call(
        conclude,
        out_shape=(
            jax.ShapeDtypeStruct((2, windows, groups, outputs), jnp.float32),
            jax.ShapeDtypeStruct((windows, outputs), jnp.float32),
        ),
        in_specs=[vmem, vmem, smem],
        out_specs=(vmem, vmem),
        name="conclude",
    )(partial, other, window_ends)

    gathered = [swap_with(settled, pairs_of(peer)) for peer in range(1, front)]

    def assemble(*args):
        return assemble_kernel(front, back, *args)

    whole = jax.ShapeDtypeStruct((windows, total_groups, outputs), jnp.float32)
    first, total = pl.pallas_call(
        assemble,
        out_shape=(whole, whole),
        in_specs=[vmem] * front,
        out_specs=(vmem, vmem),
        name="assemble",
    )(settled, *gathered)
    return first, total, variance


def solution(mesh):
    in_specs = (P(None, "rows", None), P(None, "rows", None), P(), P(), P(), P(), P("par"), P())
    out_specs = (P(None, "par", None), P(None, "par", None), P())
    return jax.shard_map(local, mesh=mesh, in_specs=in_specs, out_specs=out_specs, check_vma=False)
```

time: 133 us -> 42 us (0.32)
  blocking collectives: 52.4 us -> 0 us
  waiting for transfers between devices: 32.3 us -> 12.1 us
  between operations: 16.9 us -> 0.67 us
  Pallas kernels: 0 us -> 13.9 us
  starting transfers between devices: 0.04 us -> 11.8 us
  matrix products: 11.5 us -> 0 us
  other arithmetic: 11.5 us -> 0.74 us
  local copies, waits for them, and re-layouts: 7.03 us -> 2.51 us
    psum x1 -> x0, blocking collectives: 40.8 us -> none  [settle(): total_sum, total_squares = lax.psum(total_piece, ('rows', 'par'))]
    psum x1 -> x0, waiting for transfers between devices: 32.3 us -> none  [settle(): group_b, group_d, group_squares, group_cross = lax.psum(group_piece, 'rows')]
    pallas_call x0 -> x3, Pallas kernels: none -> 13.9 us  [the longest x1 10.6 us: local(): pl.pallas_call(evaluate, out_shape=jax.ShapeDtypeStruct((windows, height,...]
    ppermute x0 -> x7, waiting for transfers between devices: none -> 12.1 us  [swap_with(): return lax.ppermute(values, 'rows', pairs)]
    ppermute x0 -> x7, starting transfers between devices: none -> 11.8 us  [swap_with(): return lax.ppermute(values, 'rows', pairs)]
    all_gather x2 -> x0, blocking collectives: 11.7 us -> none  [the longest x1 6.23 us: local(): lax.all_gather(out_b_part, 'par', axis=1, tiled=True)]
    dot_general x5 -> x0, matrix products: 11.5 us -> none  [the longest x1 4.53 us: network_tail(): jnp.dot(hidden_one, layer_two, preferred_element_type=jnp.float32)]
    slice x7 -> x0, local copies, waits for them, and re-layouts: 3.23 us -> none  [the longest x5 2.57 us: pick_window(): return tuple((member[window:window + 1] for member in states))]
  transfers between devices with their start and end apart: 1 -> 7, of which waited for: 1 -> 5; matrix products, arithmetic and copies ran while one was open for 1% -> 0% of each run, Pallas kernels for 0% -> 0%
where the time goes in v1:
time: 42 us; the launch traced here: 41.7 us
  Pallas kernels  13.9 us (33%)
  waiting for transfers between devices  12.1 us (29%)
  starting transfers between devices  11.8 us (28%)
  local copies, waits for them, and re-layouts  2.51 us (6%)
  other arithmetic  0.74 us (2%)
  between operations  0.67 us (2%)
    ppermute x7, waiting for transfers between devices, swap_with(): return lax.ppermute(values, 'rows', pairs)  12.1 us
    ppermute x7, starting transfers between devices, swap_with(): return lax.ppermute(values, 'rows', pairs)  11.8 us
    pallas_call x1, Pallas kernels, local(): pl.pallas_call(evaluate, out_shape=jax.ShapeDtypeStruct((windows, height,...  10.6 us
    unnamed x16, local copies, waits for them, and re-layouts  2.51 us
    pallas_call x1, Pallas kernels, local(): pl.pallas_call(assemble, out_shape=(whole, whole), in_specs=[vmem] * fron...  1.66 us
    pallas_call x1, Pallas kernels, local(): pl.pallas_call(conclude, out_shape=(jax.ShapeDtypeStruct((2, windows, gro...  1.62 us
  transfers between devices with their start and end apart: 7, of which 5 were waited for; matrix products, arithmetic and copies ran while one was open for 0% of the time, Pallas kernels for 0%

profile of v1, /device:TPU:0, one launch (start us, length us, event | category | flops | bytes accessed | tf_op | source)
XLA Modules:
  0.0 41.7 jit_solution(8597371586174456133)
XLA Ops:
  0.6 0.7 %maximum_convert_fusion.args_0_ = f32[2,4,8,256]{3,2,1,0:T(8,128)S(1)} fusion(bf16[1,4,8,256]{3,2,1,0:T(8,128)(2,1)} %bitcast.3, bf16[1,4,8,256]{3,2,1,0:T(8,128)(2,1)} %bitcast.4), kind=kLoop, calls=%fused_computation | loop fusion | flops 32768 | bytes 98304 | tf_op jit(solution)/shard_map/convert_element_type | solution.py:204
  1.4 0.0 copy-start
  1.4 5.1 %collective-permute-start.2 = (f32[2,4,8,256]{3,2,1,0:T(8,128)S(1)}, f32[2,4,8,256]{3,2,1,0:T(8,128)S(1)}, u32[]{:S(2)}, u32[]{:S(2)}) collective-permute-start(f32[2,4,8,256]{3,2,1,0:T(8,128)S(1)} %maximum_convert_fusion.args_0_), channel_id=1, source_target_pairs={{24,0},{28,4},{16,8},{20,12},{8,16},{12,20},{0,24},{4,28},{25,1},{... | collective-permute-start | bytes 196616 | tf_op jit(solution)/shard_map/ppermute | solution.py:182
  6.5 0.0 collective-permute-start.1
  6.5 0.6 %collective-permute-start = (f32[2,4,8,256]{3,2,1,0:T(8,128)S(1)}, f32[2,4,8,256]{3,2,1,0:T(8,128)S(1)}, u32[]{:S(2)}, u32[]{:S(2)}) collective-permute-start(f32[2,4,8,256]{3,2,1,0:T(8,128)S(1)} %maximum_convert_fusion.args_0_), channel_id=1, source_target_pairs={{8,0},{12,4},{0,8},{4,12},{24,16},{28,20},{16,24},{20,28},{9,1},{1... | collective-permute-start | bytes 196616 | tf_op jit(solution)/shard_map/ppermute | solution.py:182
  7.2 1.8 %collective-permute-done.2.args_3_ = f32[2,4,8,256]{3,2,1,0:T(8,128)S(1)} collective-permute-done((f32[2,4,8,256]{3,2,1,0:T(8,128)S(1)}, f32[2,4,8,256]{3,2,1,0:T(8,128)S(1)}, u32[]{:S(2)}, u32[]{:S(2)}) %collective-permute-start.2) | collective-permute-done | bytes 65568 | tf_op jit(solution)/shard_map/ppermute | solution.py:182
  9.0 0.0 copy-start.2
  9.0 3.1 %collective-permute-done.1.args_2_ = f32[2,4,8,256]{3,2,1,0:T(8,128)S(1)} collective-permute-done((f32[2,4,8,256]{3,2,1,0:T(8,128)S(1)}, f32[2,4,8,256]{3,2,1,0:T(8,128)S(1)}, u32[]{:S(2)}, u32[]{:S(2)}) %collective-permute-start.1) | collective-permute-done | bytes 65568 | tf_op jit(solution)/shard_map/ppermute | solution.py:182
  12.1 0.0 copy-start.3
  12.1 0.0 collective-permute-done.args_1_
  12.1 0.0 copy-start.4
  12.1 0.0 copy-done
  12.1 0.0 copy-done.2
  12.1 0.6 %copy-done.3 = f32[2,4,8,256]{3,2,1,0:T(8,128)} copy-done((f32[2,4,8,256]{3,2,1,0:T(8,128)}, f32[2,4,8,256]{3,2,1,0:T(8,128)S(1)}, u32[]{:S(2)}) %copy-start.3) | copy-done | bytes 65560
  12.7 0.0 copy-done.4
  12.8 10.6 %evaluate.1.args_0_ = f32[4,56,128]{2,1,0:T(8,128)} custom-call(f32[2,4,8,256]{3,2,1,0:T(8,128)} %copy-done, f32[2,4,8,256]{3,2,1,0:T(8,128)} %copy-done.4, f32[2,4,8,256]{3,2,1,0:T(8,128)} %copy-done.3, f32[2,4,8,256]{3,2,1,0:T(8,128)} %copy-done.2, f32[1,256]{1,0:T(1,128)} %bitcast.5, bf16[256,1024]{1,0:T(8,128)(2,1)} %args_5_.4, ...), custom_call_target="tpu_custom_call" | custom-call | tf_op jit(solution)/shard_map/evaluate/pallas_call | solution.py:216
  23.4 1.6 %collective-permute-start.3 = (f32[4,56,128]{2,1,0:T(8,128)}, f32[4,56,128]{2,1,0:T(8,128)S(1)}, u32[]{:S(2)}, u32[]{:S(2)}) collective-permute-start(f32[4,56,128]{2,1,0:T(8,128)} %evaluate.1.args_0_), channel_id=1, source_target_pairs={{0,4},{4,0},{8,12},{12,8},{16,20},{20,16},{24,28},{28,24},{1,5},{5... | collective-permute-start | bytes 344072 | tf_op jit(solution)/shard_map/ppermute | solution.py:182
  24.9 3.5 %collective-permute-done.3.args_1_ = f32[4,56,128]{2,1,0:T(8,128)S(1)} collective-permute-done((f32[4,56,128]{2,1,0:T(8,128)}, f32[4,56,128]{2,1,0:T(8,128)S(1)}, u32[]{:S(2)}, u32[]{:S(2)}) %collective-permute-start.3) | collective-permute-done | bytes 114720 | tf_op jit(solution)/shard_map/ppermute | solution.py:182
  28.4 0.0 copy-start.1
  28.4 0.6 %copy-done.1 = f32[4,56,128]{2,1,0:T(8,128)} copy-done((f32[4,56,128]{2,1,0:T(8,128)}, f32[4,56,128]{2,1,0:T(8,128)S(1)}, u32[]{:S(2)}) %copy-start.1) | copy-done | bytes 114712
  29.1 1.6 %conclude.1 = (f32[2,4,16,128]{3,2,1,0:T(8,128)}, f32[4,128]{1,0:T(4,128)}) custom-call(f32[4,56,128]{2,1,0:T(8,128)} %evaluate.1.args_0_, f32[4,56,128]{2,1,0:T(8,128)} %copy-done.1, s32[4]{0:T(128)} %args_2_.4), custom_call_target="tpu_custom_call" | custom-call | tf_op jit(solution)/shard_map/conclude/pallas_call | solution.py:243
  30.7 2.7 %collective-permute-start.6 = (f32[2,4,16,128]{3,2,1,0:T(8,128)}, f32[2,4,16,128]{3,2,1,0:T(8,128)S(1)}, u32[]{:S(2)}, u32[]{:S(2)}) collective-permute-start(f32[2,4,16,128]{3,2,1,0:T(8,128)} %get-tuple-element.7.args_0_), channel_id=1, source_target_pairs={{24,0},{28,4},{16,8},{20,12},{8,16},{12,20},{0,24},{4,28},{25,1},{... | collective-permute-start | bytes 196616 | tf_op jit(solution)/shard_map/ppermute | solution.py:182
  33.4 0.0 collective-permute-start.5
  33.4 1.7 %collective-permute-start.4 = (f32[2,4,16,128]{3,2,1,0:T(8,128)}, f32[2,4,16,128]{3,2,1,0:T(8,128)S(1)}, u32[]{:S(2)}, u32[]{:S(2)}) collective-permute-start(f32[2,4,16,128]{3,2,1,0:T(8,128)} %get-tuple-element.7.args_0_), channel_id=1, source_target_pairs={{8,0},{12,4},{0,8},{4,12},{24,16},{28,20},{16,24},{20,28},{9,1},{1... | collective-permute-start | bytes 196616 | tf_op jit(solution)/shard_map/ppermute | solution.py:182
  35.1 2.0 %collective-permute-done.6.args_3_ = f32[2,4,16,128]{3,2,1,0:T(8,128)S(1)} collective-permute-done((f32[2,4,16,128]{3,2,1,0:T(8,128)}, f32[2,4,16,128]{3,2,1,0:T(8,128)S(1)}, u32[]{:S(2)}, u32[]{:S(2)}) %collective-permute-start.6) | collective-permute-done | bytes 65568 | tf_op jit(solution)/shard_map/ppermute | solution.py:182
  37.1 0.0 copy-start.5
  37.1 1.7 %collective-permute-done.5.args_2_ = f32[2,4,16,128]{3,2,1,0:T(8,128)S(1)} collective-permute-done((f32[2,4,16,128]{3,2,1,0:T(8,128)}, f32[2,4,16,128]{3,2,1,0:T(8,128)S(1)}, u32[]{:S(2)}, u32[]{:S(2)}) %collective-permute-start.5) | collective-permute-done | bytes 65568 | tf_op jit(solution)/shard_map/ppermute | solution.py:182
  38.8 0.0 copy-start.6
  38.8 0.0 collective-permute-done.4.args_1_
  38.8 0.0 copy-done.5
  38.8 0.6 %copy-done.6 = f32[2,4,16,128]{3,2,1,0:T(8,128)} copy-done((f32[2,4,16,128]{3,2,1,0:T(8,128)}, f32[2,4,16,128]{3,2,1,0:T(8,128)S(1)}, u32[]{:S(2)}) %copy-start.6) | copy-done | bytes 65560
  39.4 0.0 copy-start.7
  39.4 0.6 %copy-done.7 = f32[2,4,16,128]{3,2,1,0:T(8,128)} copy-done((f32[2,4,16,128]{3,2,1,0:T(8,128)}, f32[2,4,16,128]{3,2,1,0:T(8,128)S(1)}, u32[]{:S(2)}) %copy-start.7) | copy-done | bytes 65560
  40.0 1.7 %assemble.1 = (f32[4,64,128]{2,1,0:T(8,128)}, f32[4,64,128]{2,1,0:T(8,128)}) custom-call(f32[2,4,16,128]{3,2,1,0:T(8,128)} %get-tuple-element.7.args_0_, f32[2,4,16,128]{3,2,1,0:T(8,128)} %copy-done.7, f32[2,4,16,128]{3,2,1,0:T(8,128)} %copy-done.6, f32[2,4,16,128]{3,2,1,0:T(8,128)} %copy-done.5), custom_call_target="tpu_custom_call" | custom-call | tf_op jit(solution)/shard_map/assemble/pallas_call | solution.py:260
Async XLA Ops:
  1.4 10.8 %copy-start = (f32[2,4,8,256]{3,2,1,0:T(8,128)}, f32[2,4,8,256]{3,2,1,0:T(8,128)S(1)}, u32[]{:S(2)}) copy-start(f32[2,4,8,256]{3,2,1,0:T(8,128)S(1)} %maximum_convert_fusion.args_0_) | copy-start | bytes 196612
  1.4 7.6 %collective-permute-start.2 = (f32[2,4,8,256]{3,2,1,0:T(8,128)S(1)}, f32[2,4,8,256]{3,2,1,0:T(8,128)S(1)}, u32[]{:S(2)}, u32[]{:S(2)}) collective-permute-start(f32[2,4,8,256]{3,2,1,0:T(8,128)S(1)} %maximum_convert_fusion.args_0_), channel_id=1, source_target_pairs={{24,0},{28,4},{16,8},{20,12},{8,16},{12,20},{0,24},{4,28},{25,1},{... | collective-permute-start | bytes 196616 | tf_op jit(solution)/shard_map/ppermute | solution.py:182
  6.5 5.6 %collective-permute-start.1 = (f32[2,4,8,256]{3,2,1,0:T(8,128)S(1)}, f32[2,4,8,256]{3,2,1,0:T(8,128)S(1)}, u32[]{:S(2)}, u32[]{:S(2)}) collective-permute-start(f32[2,4,8,256]{3,2,1,0:T(8,128)S(1)} %maximum_convert_fusion.args_0_), channel_id=1, source_target_pairs={{16,0},{20,4},{24,8},{28,12},{0,16},{4,20},{8,24},{12,28},{17,1},{... | collective-permute-start | bytes 196616 | tf_op jit(solution)/shard_map/ppermute | solution.py:182
  6.5 5.6 %collective-permute-start = (f32[2,4,8,256]{3,2,1,0:T(8,128)S(1)}, f32[2,4,8,256]{3,2,1,0:T(8,128)S(1)}, u32[]{:S(2)}, u32[]{:S(2)}) collective-permute-start(f32[2,4,8,256]{3,2,1,0:T(8,128)S(1)} %maximum_convert_fusion.args_0_), channel_id=1, source_target_pairs={{8,0},{12,4},{0,8},{4,12},{24,16},{28,20},{16,24},{20,28},{9,1},{1... | collective-permute-start | bytes 196616 | tf_op jit(solution)/shard_map/ppermute | solution.py:182
  9.0 3.1 %copy-start.2 = (f32[2,4,8,256]{3,2,1,0:T(8,128)}, f32[2,4,8,256]{3,2,1,0:T(8,128)S(1)}, u32[]{:S(2)}) copy-start(f32[2,4,8,256]{3,2,1,0:T(8,128)S(1)} %collective-permute-done.2.args_3_) | copy-start | bytes 196612
  12.1 0.6 %copy-start.3 = (f32[2,4,8,256]{3,2,1,0:T(8,128)}, f32[2,4,8,256]{3,2,1,0:T(8,128)S(1)}, u32[]{:S(2)}) copy-start(f32[2,4,8,256]{3,2,1,0:T(8,128)S(1)} %collective-permute-done.1.args_2_) | copy-start | bytes 196612
  12.1 0.6 %copy-start.4 = (f32[2,4,8,256]{3,2,1,0:T(8,128)}, f32[2,4,8,256]{3,2,1,0:T(8,128)S(1)}, u32[]{:S(2)}) copy-start(f32[2,4,8,256]{3,2,1,0:T(8,128)S(1)} %collective-permute-done.args_1_) | copy-start | bytes 196612
  23.4 5.1 %collective-permute-start.3 = (f32[4,56,128]{2,1,0:T(8,128)}, f32[4,56,128]{2,1,0:T(8,128)S(1)}, u32[]{:S(2)}, u32[]{:S(2)}) collective-permute-start(f32[4,56,128]{2,1,0:T(8,128)} %evaluate.1.args_0_), channel_id=1, source_target_pairs={{0,4},{4,0},{8,12},{12,8},{16,20},{20,16},{24,28},{28,24},{1,5},{5... | collective-permute-start | bytes 344072 | tf_op jit(solution)/shard_map/ppermute | solution.py:182
  28.4 0.6 %copy-start.1 = (f32[4,56,128]{2,1,0:T(8,128)}, f32[4,56,128]{2,1,0:T(8,128)S(1)}, u32[]{:S(2)}) copy-start(f32[4,56,128]{2,1,0:T(8,128)S(1)} %collective-permute-done.3.args_1_) | copy-start | bytes 344068
  30.7 6.4 %collective-permute-start.6 = (f32[2,4,16,128]{3,2,1,0:T(8,128)}, f32[2,4,16,128]{3,2,1,0:T(8,128)S(1)}, u32[]{:S(2)}, u32[]{:S(2)}) collective-permute-start(f32[2,4,16,128]{3,2,1,0:T(8,128)} %get-tuple-element.7.args_0_), channel_id=1, source_target_pairs={{24,0},{28,4},{16,8},{20,12},{8,16},{12,20},{0,24},{4,28},{25,1},{... | collective-permute-start | bytes 196616 | tf_op jit(solution)/shard_map/ppermute | solution.py:182
  33.4 5.4 %collective-permute-start.5 = (f32[2,4,16,128]{3,2,1,0:T(8,128)}, f32[2,4,16,128]{3,2,1,0:T(8,128)S(1)}, u32[]{:S(2)}, u32[]{:S(2)}) collective-permute-start(f32[2,4,16,128]{3,2,1,0:T(8,128)} %get-tuple-element.7.args_0_), channel_id=1, source_target_pairs={{16,0},{20,4},{24,8},{28,12},{0,16},{4,20},{8,24},{12,28},{17,1},{... | collective-permute-start | bytes 196616 | tf_op jit(solution)/shard_map/ppermute | solution.py:182
  33.4 5.4 %collective-permute-start.4 = (f32[2,4,16,128]{3,2,1,0:T(8,128)}, f32[2,4,16,128]{3,2,1,0:T(8,128)S(1)}, u32[]{:S(2)}, u32[]{:S(2)}) collective-permute-start(f32[2,4,16,128]{3,2,1,0:T(8,128)} %get-tuple-element.7.args_0_), channel_id=1, source_target_pairs={{8,0},{12,4},{0,8},{4,12},{24,16},{28,20},{16,24},{20,28},{9,1},{1... | collective-permute-start | bytes 196616 | tf_op jit(solution)/shard_map/ppermute | solution.py:182
  37.1 1.7 %copy-start.5 = (f32[2,4,16,128]{3,2,1,0:T(8,128)}, f32[2,4,16,128]{3,2,1,0:T(8,128)S(1)}, u32[]{:S(2)}) copy-start(f32[2,4,16,128]{3,2,1,0:T(8,128)S(1)} %collective-permute-done.6.args_3_) | copy-start | bytes 196612
  38.8 0.6 %copy-start.6 = (f32[2,4,16,128]{3,2,1,0:T(8,128)}, f32[2,4,16,128]{3,2,1,0:T(8,128)S(1)}, u32[]{:S(2)}) copy-start(f32[2,4,16,128]{3,2,1,0:T(8,128)S(1)} %collective-permute-done.5.args_2_) | copy-start | bytes 196612
  39.4 0.6 %copy-start.7 = (f32[2,4,16,128]{3,2,1,0:T(8,128)}, f32[2,4,16,128]{3,2,1,0:T(8,128)S(1)}, u32[]{:S(2)}) copy-start(f32[2,4,16,128]{3,2,1,0:T(8,128)S(1)} %collective-permute-done.4.args_1_) | copy-start | bytes 196612

commit v2 on v1

v2 whole, which is shorter than its diff:
```python
import math

import jax
import jax.numpy as jnp
from jax import lax
from jax.experimental import pallas as pl
from jax.experimental.pallas import tpu as pltpu
from jax.sharding import PartitionSpec as P

CHUNK_ROWS = 576
COLUMN_TILE = 256
SPARE_BYTES = 10 * 1024 * 1024


def dot(left, right):
    return jnp.dot(left, right, preferred_element_type=jnp.float32)


def silu_half(half):
    return half + half * jnp.tanh(half)


def units_per_chunk(units, rows):
    return max(count for count in range(1, units + 1) if units % count == 0 and (count == 1 or count * rows <= CHUNK_ROWS))


def member_of(place, peer, front):
    return jnp.bitwise_xor(place, peer) if front & (front - 1) == 0 else lax.rem(place + peer, front)


def networks(pieces, mask_of, scale, picks, one_ref, wait_one, two_ref, three_ref, wait_rest, base_sums, out_ref, scratch):
    pre_ref, first_ref, second_ref, result_ref, base_ref = scratch
    windows, block_rows, width = pieces[0].shape[1:]
    groups = picks.shape[0]
    hidden = one_ref.shape[1]
    outputs = three_ref.shape[1]
    rows = len(pieces) * windows * block_rows

    def scaled(which):
        return jnp.concatenate(
            [(piece[which].reshape(windows * block_rows, width) * scale).astype(jnp.bfloat16) for piece in pieces], 0
        )

    inputs_a = scaled(0)
    inputs_b = scaled(1)
    contract = (((1,), (1,)), ((), ()))
    delta = 0.5 * (
        lax.dot_general(inputs_b, picks, contract, preferred_element_type=jnp.float32)
        - lax.dot_general(inputs_a, picks, contract, preferred_element_type=jnp.float32)
    )
    wait_one()
    picked = dot(picks, one_ref[...])
    inputs_ab = jnp.concatenate([inputs_a, inputs_b], 0)
    for start in range(0, hidden, COLUMN_TILE):
        tile = slice(start, start + COLUMN_TILE)
        pre_ref[:, tile] = 0.5 * dot(inputs_ab, one_ref[:, tile])

    units = groups + 2
    per_chunk = units_per_chunk(units, rows)

    def fill(chunk):
        for index in range(per_chunk):
            unit = chunk * per_chunk + index
            for start in range(0, hidden, COLUMN_TILE):
                tile = slice(start, start + COLUMN_TILE)
                half = pre_ref[rows : 2 * rows, tile] if unit == 1 else pre_ref[:rows, tile]
                if unit >= 2:
                    group = unit - 2
                    half = half + delta[:, group : group + 1] * picked[group : group + 1, tile]
                first_ref[chunk % 2, index * rows : (index + 1) * rows, tile] = silu_half(half).astype(jnp.bfloat16)

    def tail(chunk):
        for start in range(0, hidden, COLUMN_TILE):
            tile = slice(start, start + COLUMN_TILE)
            half = 0.5 * dot(first_ref[chunk % 2], two_ref[:, tile])
            second_ref[chunk % 2, :, tile] = silu_half(half).astype(jnp.bfloat16)
        return dot(second_ref[chunk % 2], three_ref[...])

    def block_at(peer, window):
        return (peer * windows + window) * block_rows

    def total(value):
        return jnp.sum(value, axis=0, keepdims=True)

    chunks = units // per_chunk
    fill(0)
    wait_rest()
    for chunk in range(chunks):
        if chunk + 1 < chunks:
            fill(chunk + 1)
        result_ref[chunk % 2] = tail(chunk)
        for index in range(per_chunk):
            unit = chunk * per_chunk + index
            if unit < 2:
                base_ref[unit] = result_ref[chunk % 2, index * rows : (index + 1) * rows]
                if unit == 1:
                    for window in range(windows):
                        sums = [jnp.zeros((block_rows, outputs), jnp.float32) for _ in range(3)]
                        for peer in range(len(pieces)):
                            mask = mask_of(peer, window)
                            at = block_at(peer, window)
                            va = base_ref[0, at : at + block_rows]
                            vb = base_ref[1, at : at + block_rows]
                            sums[0] += mask * vb
                            sums[1] += mask * (va + vb)
                            sums[2] += mask * (va * va + vb * vb)
                        base_sums(window, [total(value) for value in sums])
                continue
            group = unit - 2
            for window in range(windows):
                sums = [jnp.zeros((block_rows, outputs), jnp.float32) for _ in range(3)]
                for peer in range(len(pieces)):
                    at = block_at(peer, window)
                    here = index * rows + at
                    differ = result_ref[chunk % 2, here : here + block_rows] - base_ref[0, at : at + block_rows]
                    masked = mask_of(peer, window) * differ
                    sums[0] += masked
                    sums[1] += masked * differ
                    sums[2] += masked * base_ref[1, at : at + block_rows]
                for kind in range(3):
                    out_ref(window, kind * groups + group, total(sums[kind]))


def early_kernel(
    front, back, own_ref, scale_hbm, one_hbm, two_hbm, three_hbm, cols_hbm, ends_hbm,
    out_ref, scale_ref, one_ref, two_ref, three_ref, picks_ref, masks_ref, cols_ref, ends_ref, sems, *scratch,
):
    moves = (
        (cols_hbm, cols_ref),
        (ends_hbm, ends_ref),
        (scale_hbm, scale_ref),
        (one_hbm, one_ref),
        (two_hbm, two_ref),
        (three_hbm, three_ref),
    )
    copies = [pltpu.make_async_copy(source, target, sems.at[index]) for index, (source, target) in enumerate(moves)]
    for copy in copies:
        copy.start()
    for copy in copies[:3]:
        copy.wait()
    windows, block_rows, width = own_ref.shape[1:]
    groups = picks_ref.shape[0]
    outputs = three_ref.shape[1]
    device = lax.axis_index("rows")
    place = device // back
    corner = device % back
    row_ids = lax.broadcasted_iota(jnp.int32, (groups, width), 0)
    lane_ids = lax.broadcasted_iota(jnp.int32, (groups, width), 1)
    wanted = jnp.zeros((groups, width), jnp.int32)
    for group in range(groups):
        wanted = jnp.where(row_ids == group, cols_ref[place * groups + group], wanted)
    picks = jnp.where(lane_ids == wanted, 1.0, 0.0).astype(jnp.bfloat16)
    picks_ref[...] = picks
    sublane = lax.broadcasted_iota(jnp.int32, (block_rows, outputs), 0)
    own_masks = []
    for peer in range(front):
        first_row = (member_of(place, peer, front) * back + corner) * block_rows
        for window in range(windows):
            mask = jnp.where(sublane + first_row < ends_ref[window], 1.0, 0.0)
            if peer == 0:
                own_masks.append(mask)
            else:
                masks_ref[peer - 1, window] = mask
    counts = []
    count = jnp.int32(0)
    for window in range(windows):
        count = count + ends_ref[window]
        counts.append(count)

    def base_sums(window, lines):
        lines = lines + [jnp.zeros((1, outputs), jnp.float32) + counts[window].astype(jnp.float32)]
        lines.append(jnp.zeros((8 - len(lines), outputs), jnp.float32))
        out_ref[window, 3 * groups :, :] = jnp.concatenate(lines, 0)

    def store(window, line, value):
        out_ref[window, line : line + 1, :] = value

    def wait_rest():
        copies[4].wait()
        copies[5].wait()

    networks(
        [own_ref], lambda peer, window: own_masks[window], scale_ref[...], picks, one_ref, copies[3].wait,
        two_ref, three_ref, wait_rest, base_sums, store, scratch,
    )


def late_kernel(front, *refs):
    pieces = refs[: front - 1]
    scale_ref, one_ref, two_ref, three_ref, picks_ref, masks_ref, early_ref, out_ref = refs[front - 1 : front + 7]
    scratch = refs[front + 7 :]
    groups = picks_ref.shape[0]

    def base_sums(window, lines):
        for index, line in enumerate(lines):
            store(window, 3 * groups + index, line)
        rest = slice(3 * groups + len(lines), None)
        out_ref[window, rest, :] = early_ref[window, rest, :]

    def store(window, line, value):
        out_ref[window, line : line + 1, :] = early_ref[window, line : line + 1, :] + value

    def nothing():
        return None

    networks(
        list(pieces), lambda peer, window: masks_ref[peer, window], scale_ref[...], picks_ref[...], one_ref, nothing,
        two_ref, three_ref, nothing, base_sums, store, scratch,
    )


def conclude_kernel(groups, own_ref, other_ref, out_ref, variance_ref):
    windows = own_ref.shape[0]
    running = jnp.zeros(own_ref.shape[1:], jnp.float32)
    for window in range(windows):
        running = running + (own_ref[window] + other_ref[window])
        share = 1.0 / own_ref[window, 3 * groups + 3 : 3 * groups + 4]
        sum_b = running[3 * groups : 3 * groups + 1]
        sum_all = running[3 * groups + 1 : 3 * groups + 2]
        squares = running[3 * groups + 2 : 3 * groups + 3]
        mean = sum_all * (0.5 * share)
        variance = (squares - sum_all * mean) * (0.5 * share)
        mean_d = running[:groups] * share
        weight = share / variance
        out_ref[0, window] = (running[2 * groups : 3 * groups] - sum_b * mean_d) * weight
        out_ref[1, window] = running[groups : 2 * groups] * (0.5 * weight)
        variance_ref[window : window + 1, :] = variance


def assemble_kernel(front, back, own_ref, *refs):
    peers = refs[: front - 1]
    settled_ref, first_ref, total_ref, variance_ref = refs[front - 1 :]
    place = lax.axis_index("rows") // back
    groups = own_ref.shape[2]
    for peer, ref in enumerate([own_ref] + list(peers)):
        start = pl.multiple_of(member_of(place, peer, front) * groups, groups)
        first_ref[:, pl.ds(start, groups), :] = ref[0]
        total_ref[:, pl.ds(start, groups), :] = ref[1]
    variance_ref[...] = settled_ref[...]


def near(values):
    return pltpu.with_memory_space_constraint(values, pltpu.VMEM)


def far(values):
    return pltpu.with_memory_space_constraint(values, pltpu.HBM)


def exchange(values, pairs):
    return lax.ppermute(values, "rows", pairs)


def local(base_a, base_b, input_scale, layer_one, layer_two, layer_three, swap_cols, window_ends):
    windows, block_rows, width = base_a.shape
    size = lax.axis_size("rows")
    total_groups = swap_cols.shape[0]
    hidden = layer_one.shape[1]
    outputs = layer_three.shape[1]
    back = 2 if size % 2 == 0 else 1
    front = size // back
    groups = total_groups // front
    height = 3 * groups + 8

    def pairs_of(peer):
        pairs = []
        for device in range(size):
            place, corner = divmod(device, back)
            source = (place ^ peer) if front & (front - 1) == 0 else (place + peer) % front
            pairs.append((source * back + corner, device))
        return pairs

    vmem = pl.BlockSpec(memory_space=pltpu.VMEM)
    anywhere = pl.BlockSpec(memory_space=pl.ANY)

    def scratch_of(count):
        rows = count * windows * block_rows
        chunk = units_per_chunk(groups + 2, rows) * rows
        return [
            pltpu.VMEM((2 * rows, hidden), jnp.float32),
            pltpu.VMEM((2, chunk, hidden), jnp.bfloat16),
            pltpu.VMEM((2, chunk, hidden), jnp.bfloat16),
            pltpu.VMEM((2, chunk, outputs), jnp.float32),
            pltpu.VMEM((2, rows, outputs), jnp.float32),
        ]

    def room_of(count):
        held = sum(math.prod(space.shape) * jnp.dtype(space.dtype).itemsize for space in scratch_of(count))
        return pltpu.CompilerParams(vmem_limit_bytes=held + SPARE_BYTES)

    def work_of(count):
        rows = count * windows * block_rows * (groups + 2)
        return pl.CostEstimate(
            flops=2 * rows * hidden * (hidden + outputs),
            transcendentals=2 * rows * hidden,
            bytes_accessed=2 * (layer_one.size + layer_two.size + layer_three.size),
        )

    own = jnp.stack([base_a, base_b]).astype(jnp.float32)
    received = [exchange(own, pairs_of(peer)) for peer in range(1, front)]
    scale = input_scale.reshape(1, width)

    def early(*args):
        return early_kernel(front, back, *args)

    sums, scales, one, two, three, picks, masks = pl.pallas_call(
        early,
        out_shape=(
            pltpu.VMEM((windows, height, outputs), jnp.float32),
            pltpu.VMEM(scale.shape, scale.dtype),
            pltpu.VMEM(layer_one.shape, layer_one.dtype),
            pltpu.VMEM(layer_two.shape, layer_two.dtype),
            pltpu.VMEM(layer_three.shape, layer_three.dtype),
            pltpu.VMEM((groups, width), jnp.bfloat16),
            pltpu.VMEM((front - 1, windows, block_rows, outputs), jnp.float32),
        ),
        in_specs=[vmem] + [anywhere] * 6,
        out_specs=(vmem,) * 7,
        scratch_shapes=[
            pltpu.SMEM(swap_cols.shape, swap_cols.dtype),
            pltpu.SMEM(window_ends.shape, window_ends.dtype),
            pltpu.SemaphoreType.DMA((6,)),
            *scratch_of(1),
        ],
        cost_estimate=work_of(1),
        compiler_params=room_of(1),
        name="early",
    )(near(own), *(far(value) for value in (scale, layer_one, layer_two, layer_three, swap_cols, window_ends)))

    def late(*args):
        return late_kernel(front, *args)

    partial = pl.pallas_call(
        late,
        out_shape=pltpu.VMEM((windows, height, outputs), jnp.float32),
        in_specs=[vmem] * (front + 6),
        out_specs=vmem,
        scratch_shapes=scratch_of(front - 1),
        cost_estimate=work_of(front - 1),
        compiler_params=room_of(front - 1),
        name="late",
    )(*(near(value) for value in (*received, scales, one, two, three, picks, masks, sums)))

    if back == 2:
        other = exchange(partial, [(device, device ^ 1) for device in range(size)])
    else:
        other = jnp.zeros_like(partial)

    def conclude(*args):
        return conclude_kernel(groups, *args)

    settled, variance = pl.pallas_call(
        conclude,
        out_shape=(
            pltpu.VMEM((2, windows, groups, outputs), jnp.float32),
            pltpu.VMEM((windows, outputs), jnp.float32),
        ),
        in_specs=[vmem, vmem],
        out_specs=(vmem, vmem),
        compiler_params=pltpu.CompilerParams(vmem_limit_bytes=SPARE_BYTES),
        name="conclude",
    )(near(partial), near(other))

    gathered = [exchange(settled, pairs_of(peer)) for peer in range(1, front)]

    def assemble(*args):
        return assemble_kernel(front, back, *args)

    whole = jax.ShapeDtypeStruct((windows, total_groups, outputs), jnp.float32)
    return pl.pallas_call(
        assemble,
        out_shape=(whole, whole, jax.ShapeDtypeStruct((windows, outputs), jnp.float32)),
        in_specs=[vmem] * (front + 1),
        out_specs=(vmem, vmem, vmem),
        compiler_params=pltpu.CompilerParams(vmem_limit_bytes=SPARE_BYTES),
        name="assemble",
    )(*(near(value) for value in (settled, *gathered, variance)))


def solution(mesh):
    in_specs = (P(None, "rows", None), P(None, "rows", None), P(), P(), P(), P(), P("par"), P())
    out_specs = (P(None, "par", None), P(None, "par", None), P())
    return jax.shard_map(local, mesh=mesh, in_specs=in_specs, out_specs=out_specs, check_vma=False)
```

time: 42 us -> 31.9 us (0.76)
  waiting for transfers between devices: 12.1 us -> 7.9 us
  Pallas kernels: 13.9 us -> 10.5 us
  local copies, waits for them, and re-layouts: 2.51 us -> 0 us
    ppermute x7, waiting for transfers between devices: 12.1 us -> 7.9 us  [exchange(): return lax.ppermute(values, 'rows', pairs)]
    pallas_call x3 -> x4, Pallas kernels: 13.9 us -> 10.5 us  [the longest x1 5.91 us: local(): pl.pallas_call(late, out_shape=pltpu.VMEM((windows, height, outputs), jnp...]
    unnamed x16 -> x0, local copies, waits for them, and re-layouts: 2.51 us -> none
  transfers between devices with their start and end apart: 7 -> 7, of which waited for: 5 -> 4; matrix products, arithmetic and copies ran while one was open for 0% -> 0% of each run, Pallas kernels for 0% -> 12%
where the time goes in v2:
time: 31.9 us; the launch traced here: 31.6 us
  starting transfers between devices  11.8 us (37%)
  Pallas kernels  10.5 us (33%)
  waiting for transfers between devices  7.9 us (25%)
  other arithmetic  0.74 us (2%)
  between operations  0.66 us (2%)
    ppermute x7, starting transfers between devices, exchange(): return lax.ppermute(values, 'rows', pairs)  11.8 us
    ppermute x7, waiting for transfers between devices, exchange(): return lax.ppermute(values, 'rows', pairs)  7.9 us
    pallas_call x1, Pallas kernels, local(): pl.pallas_call(late, out_shape=pltpu.VMEM((windows, height, outputs), jnp...  5.91 us
    pallas_call x1, Pallas kernels, local(): pl.pallas_call(early, out_shape=(pltpu.VMEM((windows, height, outputs), j...  3.82 us
    convert_element_type x1, other arithmetic, local(): own = jnp.stack([base_a, base_b]).astype(jnp.float32)  0.74 us
    pallas_call x1, Pallas kernels, local(): pl.pallas_call(assemble, out_shape=(whole, whole, jax.ShapeDtypeStruct((w...  0.73 us
  transfers between devices with their start and end apart: 7, of which 4 were waited for; matrix products, arithmetic and copies ran while one was open for 0% of the time, Pallas kernels for 12%

profile of v2, /device:TPU:0, one launch (start us, length us, event | category | flops | bytes accessed | tf_op | source)
XLA Modules:
  0.0 31.6 jit_solution(18120108770506532640)
XLA Ops:
  0.6 0.7 %maximum_convert_fusion.args_0_ = f32[2,4,8,256]{3,2,1,0:T(8,128)S(1)} fusion(bf16[1,4,8,256]{3,2,1,0:T(8,128)(2,1)} %bitcast.3, bf16[1,4,8,256]{3,2,1,0:T(8,128)(2,1)} %bitcast.4), kind=kLoop, calls=%fused_computation | loop fusion | flops 32768 | bytes 98304 | tf_op jit(solution)/shard_map/convert_element_type | solution.py:299
  1.4 5.1 %collective-permute-start.2 = (f32[2,4,8,256]{3,2,1,0:T(8,128)S(1)}, f32[2,4,8,256]{3,2,1,0:T(8,128)S(1)}, u32[]{:S(2)}, u32[]{:S(2)}) collective-permute-start(f32[2,4,8,256]{3,2,1,0:T(8,128)S(1)} %maximum_convert_fusion.args_0_), channel_id=1, source_target_pairs={{24,0},{28,4},{16,8},{20,12},{8,16},{12,20},{0,24},{4,28},{25,1},{... | collective-permute-start | bytes 196616 | tf_op jit(solution)/shard_map/ppermute | solution.py:251
  6.5 0.0 collective-permute-start.1
  6.5 0.6 %collective-permute-start = (f32[2,4,8,256]{3,2,1,0:T(8,128)S(1)}, f32[2,4,8,256]{3,2,1,0:T(8,128)S(1)}, u32[]{:S(2)}, u32[]{:S(2)}) collective-permute-start(f32[2,4,8,256]{3,2,1,0:T(8,128)S(1)} %maximum_convert_fusion.args_0_), channel_id=1, source_target_pairs={{8,0},{12,4},{0,8},{4,12},{24,16},{28,20},{16,24},{20,28},{9,1},{1... | collective-permute-start | bytes 196616 | tf_op jit(solution)/shard_map/ppermute | solution.py:251
  7.1 3.8 %early.1 = (f32[4,56,128]{2,1,0:T(8,128)S(1)}, f32[1,256]{1,0:T(1,128)S(1)}, bf16[256,1024]{1,0:T(8,128)(2,1)S(1)}, bf16[1024,1024]{1,0:T(8,128)(2,1)S(1)}, bf16...) custom-call(f32[2,4,8,256]{3,2,1,0:T(8,128)S(1)} %maximum_convert_fusion.args_0_, ...), custom_call_target="tpu_custom_call" | custom-call | flops 1358954496 | bytes 2883584 | tf_op jit(solution)/shard_map/early/pallas_call | solution.py:306
  11.0 0.0 collective-permute-done.2.args_2_
  11.0 1.1 %collective-permute-done.1.args_1_ = f32[2,4,8,256]{3,2,1,0:T(8,128)S(1)} collective-permute-done((f32[2,4,8,256]{3,2,1,0:T(8,128)S(1)}, f32[2,4,8,256]{3,2,1,0:T(8,128)S(1)}, u32[]{:S(2)}, u32[]{:S(2)}) %collective-permute-start.1) | collective-permute-done | bytes 65568 | tf_op jit(solution)/shard_map/ppermute | solution.py:251
  12.1 0.0 collective-permute-done.args_0_
  12.1 5.9 %late.1.args_0_ = f32[4,56,128]{2,1,0:T(8,128)S(1)} custom-call(f32[2,4,8,256]{3,2,1,0:T(8,128)S(1)} %collective-permute-done.args_0_, f32[2,4,8,256]{3,2,1,0:T(8,128)S(1)} %collective-permute-done.1.args_1_, f32[2,4,8,256]{3,2,1,0:T(8,128)S(1)} %collective-permute-done.2.args_2_, f32[1,256]{1,0:T(1,128)S(1)} %get-tuple-element.12.args_3_, ...), custom_call_target="tpu_custom_call" | custom-call | flops 4076863488 | bytes 2883584 | tf_op jit(solution)/shard_map/late/pallas_call | solution.py:333
  18.0 1.6 %collective-permute-start.3 = (f32[4,56,128]{2,1,0:T(8,128)S(1)}, f32[4,56,128]{2,1,0:T(8,128)S(1)}, u32[]{:S(2)}, u32[]{:S(2)}) collective-permute-start(f32[4,56,128]{2,1,0:T(8,128)S(1)} %late.1.args_0_), channel_id=1, source_target_pairs={{0,4},{4,0},{8,12},{12,8},{16,20},{20,16},{24,28},{28,24},{1,5},{5... | collective-permute-start | bytes 344072 | tf_op jit(solution)/shard_map/ppermute | solution.py:251
  19.6 3.3 %collective-permute-done.3.args_1_ = f32[4,56,128]{2,1,0:T(8,128)S(1)} collective-permute-done((f32[4,56,128]{2,1,0:T(8,128)S(1)}, f32[4,56,128]{2,1,0:T(8,128)S(1)}, u32[]{:S(2)}, u32[]{:S(2)}) %collective-permute-start.3) | collective-permute-done | bytes 114720 | tf_op jit(solution)/shard_map/ppermute | solution.py:251
  22.9 2.8 %collective-permute-start.6 = (f32[2,4,16,128]{3,2,1,0:T(8,128)S(1)}, f32[2,4,16,128]{3,2,1,0:T(8,128)S(1)}, u32[]{:S(2)}, u32[]{:S(2)}) collective-permute-start(f32[2,4,16,128]{3,2,1,0:T(8,128)S(1)} %get-tuple-element.19.args_0_), channel_id=1, source_target_pairs={{24,0},{28,4},{16,8},{20,12},{8,16},{12,20},{0,24},{4,28},{25,1},{... | collective-permute-start | bytes 196616 | tf_op jit(solution)/shard_map/ppermute | solution.py:251
  25.7 0.0 collective-permute-start.5
  25.7 1.7 %collective-permute-start.4 = (f32[2,4,16,128]{3,2,1,0:T(8,128)S(1)}, f32[2,4,16,128]{3,2,1,0:T(8,128)S(1)}, u32[]{:S(2)}, u32[]{:S(2)}) collective-permute-start(f32[2,4,16,128]{3,2,1,0:T(8,128)S(1)} %get-tuple-element.19.args_0_), channel_id=1, source_target_pairs={{8,0},{12,4},{0,8},{4,12},{24,16},{28,20},{16,24},{20,28},{9,1},{1... | collective-permute-start | bytes 196616 | tf_op jit(solution)/shard_map/ppermute | solution.py:251
  27.4 2.0 %collective-permute-done.6.args_3_ = f32[2,4,16,128]{3,2,1,0:T(8,128)S(1)} collective-permute-done((f32[2,4,16,128]{3,2,1,0:T(8,128)S(1)}, f32[2,4,16,128]{3,2,1,0:T(8,128)S(1)}, u32[]{:S(2)}, u32[]{:S(2)}) %collective-permute-start.6) | collective-permute-done | bytes 65568 | tf_op jit(solution)/shard_map/ppermute | solution.py:251
  29.4 1.5 %collective-permute-done.5.args_2_ = f32[2,4,16,128]{3,2,1,0:T(8,128)S(1)} collective-permute-done((f32[2,4,16,128]{3,2,1,0:T(8,128)S(1)}, f32[2,4,16,128]{3,2,1,0:T(8,128)S(1)}, u32[]{:S(2)}, u32[]{:S(2)}) %collective-permute-start.5) | collective-permute-done | bytes 65568 | tf_op jit(solution)/shard_map/ppermute | solution.py:251
  30.9 0.0 collective-permute-done.4.args_1_
  30.9 0.7 %assemble.1 = (f32[4,64,128]{2,1,0:T(8,128)}, f32[4,64,128]{2,1,0:T(8,128)}, f32[4,128]{1,0:T(4,128)}) custom-call(f32[2,4,16,128]{3,2,1,0:T(8,128)S(1)} %get-tuple-element.19.args_0_, f32[2,4,16,128]{3,2,1,0:T(8,128)S(1)} %collective-permute-done.4.args_1_, f32[2,4,16,128]{3,2,1,0:T(8,128)S(1)} %collective-permute-done.5.args_2_, ...), custom_call_target="tpu_custom_call" | custom-call | tf_op jit(solution)/shard_map/assemble/pallas_call | solution.py:370
  (1 shorter events, 0.0 us)
Async XLA Ops:
  1.4 9.6 %collective-permute-start.2 = (f32[2,4,8,256]{3,2,1,0:T(8,128)S(1)}, f32[2,4,8,256]{3,2,1,0:T(8,128)S(1)}, u32[]{:S(2)}, u32[]{:S(2)}) collective-permute-start(f32[2,4,8,256]{3,2,1,0:T(8,128)S(1)} %maximum_convert_fusion.args_0_), channel_id=1, source_target_pairs={{24,0},{28,4},{16,8},{20,12},{8,16},{12,20},{0,24},{4,28},{25,1},{... | collective-permute-start | bytes 196616 | tf_op jit(solution)/shard_map/ppermute | solution.py:251
  6.5 5.6 %collective-permute-start.1 = (f32[2,4,8,256]{3,2,1,0:T(8,128)S(1)}, f32[2,4,8,256]{3,2,1,0:T(8,128)S(1)}, u32[]{:S(2)}, u32[]{:S(2)}) collective-permute-start(f32[2,4,8,256]{3,2,1,0:T(8,128)S(1)} %maximum_convert_fusion.args_0_), channel_id=1, source_target_pairs={{16,0},{20,4},{24,8},{28,12},{0,16},{4,20},{8,24},{12,28},{17,1},{... | collective-permute-start | bytes 196616 | tf_op jit(solution)/shard_map/ppermute | solution.py:251
  6.5 5.6 %collective-permute-start = (f32[2,4,8,256]{3,2,1,0:T(8,128)S(1)}, f32[2,4,8,256]{3,2,1,0:T(8,128)S(1)}, u32[]{:S(2)}, u32[]{:S(2)}) collective-permute-start(f32[2,4,8,256]{3,2,1,0:T(8,128)S(1)} %maximum_convert_fusion.args_0_), channel_id=1, source_target_pairs={{8,0},{12,4},{0,8},{4,12},{24,16},{28,20},{16,24},{20,28},{9,1},{1... | collective-permute-start | bytes 196616 | tf_op jit(solution)/shard_map/ppermute | solution.py:251
  18.0 4.9 %collective-permute-start.3 = (f32[4,56,128]{2,1,0:T(8,128)S(1)}, f32[4,56,128]{2,1,0:T(8,128)S(1)}, u32[]{:S(2)}, u32[]{:S(2)}) collective-permute-start(f32[4,56,128]{2,1,0:T(8,128)S(1)} %late.1.args_0_), channel_id=1, source_target_pairs={{0,4},{4,0},{8,12},{12,8},{16,20},{20,16},{24,28},{28,24},{1,5},{5... | collective-permute-start | bytes 344072 | tf_op jit(solution)/shard_map/ppermute | solution.py:251
  22.9 6.4 %collective-permute-start.6 = (f32[2,4,16,128]{3,2,1,0:T(8,128)S(1)}, f32[2,4,16,128]{3,2,1,0:T(8,128)S(1)}, u32[]{:S(2)}, u32[]{:S(2)}) collective-permute-start(f32[2,4,16,128]{3,2,1,0:T(8,128)S(1)} %get-tuple-element.19.args_0_), channel_id=1, source_target_pairs={{24,0},{28,4},{16,8},{20,12},{8,16},{12,20},{0,24},{4,28},{25,1},{... | collective-permute-start | bytes 196616 | tf_op jit(solution)/shard_map/ppermute | solution.py:251
  25.7 5.2 %collective-permute-start.5 = (f32[2,4,16,128]{3,2,1,0:T(8,128)S(1)}, f32[2,4,16,128]{3,2,1,0:T(8,128)S(1)}, u32[]{:S(2)}, u32[]{:S(2)}) collective-permute-start(f32[2,4,16,128]{3,2,1,0:T(8,128)S(1)} %get-tuple-element.19.args_0_), channel_id=1, source_target_pairs={{16,0},{20,4},{24,8},{28,12},{0,16},{4,20},{8,24},{12,28},{17,1},{... | collective-permute-start | bytes 196616 | tf_op jit(solution)/shard_map/ppermute | solution.py:251
  25.7 5.2 %collective-permute-start.4 = (f32[2,4,16,128]{3,2,1,0:T(8,128)S(1)}, f32[2,4,16,128]{3,2,1,0:T(8,128)S(1)}, u32[]{:S(2)}, u32[]{:S(2)}) collective-permute-start(f32[2,4,16,128]{3,2,1,0:T(8,128)S(1)} %get-tuple-element.19.args_0_), channel_id=1, source_target_pairs={{8,0},{12,4},{0,8},{4,12},{24,16},{28,20},{16,24},{20,28},{9,1},{1... | collective-permute-start | bytes 196616 | tf_op jit(solution)/shard_map/ppermute | solution.py:251

commit v3 on v2

v3 whole, which is shorter than its diff:
```python
import math

import jax
import jax.numpy as jnp
from jax import lax
from jax.experimental import pallas as pl
from jax.experimental.pallas import tpu as pltpu
from jax.sharding import PartitionSpec as P

CHUNK_ROWS = 576
COLUMN_TILE = 256
PASS_FLOPS = 4_000_000_000
SPARE_BYTES = 10 * 1024 * 1024


def dot(left, right):
    return jnp.dot(left, right, preferred_element_type=jnp.float32)


def silu_half(half):
    return half + half * jnp.tanh(half)


def units_per_chunk(units, rows):
    return max(count for count in range(1, units + 1) if units % count == 0 and (count == 1 or count * rows <= CHUNK_ROWS))


def member_of(place, peer, front):
    return jnp.bitwise_xor(place, peer) if front & (front - 1) == 0 else lax.rem(place + peer, front)


def total(value):
    return jnp.sum(value, axis=0, keepdims=True)


def prepare(pieces, scale, picks, one_ref, pre_ref):
    windows, block_rows, width = pieces[0].shape[1:]
    hidden = one_ref.shape[1]

    def scaled(which):
        return jnp.concatenate(
            [(piece[which].reshape(windows * block_rows, width) * scale).astype(jnp.bfloat16) for piece in pieces], 0
        )

    inputs_a = scaled(0)
    inputs_b = scaled(1)
    contract = (((1,), (1,)), ((), ()))
    delta = 0.5 * (
        lax.dot_general(inputs_b, picks, contract, preferred_element_type=jnp.float32)
        - lax.dot_general(inputs_a, picks, contract, preferred_element_type=jnp.float32)
    )
    picked = dot(picks, one_ref[...])
    inputs_ab = jnp.concatenate([inputs_a, inputs_b], 0)
    for start in range(0, hidden, COLUMN_TILE):
        tile = slice(start, start + COLUMN_TILE)
        pre_ref[:, tile] = 0.5 * dot(inputs_ab, one_ref[:, tile])
    return delta, picked


def fill(units, rows, pre_ref, delta, picked, filled_ref):
    hidden = pre_ref.shape[1]
    for index, unit in enumerate(units):
        for start in range(0, hidden, COLUMN_TILE):
            tile = slice(start, start + COLUMN_TILE)
            half = pre_ref[rows : 2 * rows, tile] if unit == 1 else pre_ref[:rows, tile]
            if unit >= 2:
                group = unit - 2
                half = half + delta[:, group : group + 1] * picked[group : group + 1, tile]
            filled_ref[index * rows : (index + 1) * rows, tile] = silu_half(half).astype(jnp.bfloat16)


def tail(filled_ref, second_ref, two_ref, three_ref):
    hidden = two_ref.shape[1]
    for start in range(0, hidden, COLUMN_TILE):
        tile = slice(start, start + COLUMN_TILE)
        half = 0.5 * dot(filled_ref[...], two_ref[:, tile])
        second_ref[:, tile] = silu_half(half).astype(jnp.bfloat16)
    return dot(second_ref[...], three_ref[...])


def tally(units, count, windows, block_rows, mask_of, result_ref, base_ref, base_sums, store):
    outputs = result_ref.shape[1]
    rows = count * windows * block_rows
    zero = jnp.zeros((block_rows, outputs), jnp.float32)
    for index, unit in enumerate(units):
        if unit < 2:
            base_ref[unit] = result_ref[index * rows : (index + 1) * rows]
            if unit == 0:
                continue
        for window in range(windows):
            sums = [zero, zero, zero]
            for peer in range(count):
                at = (peer * windows + window) * block_rows
                mask = mask_of(peer, window)
                va = base_ref[0, at : at + block_rows]
                vb = base_ref[1, at : at + block_rows]
                if unit == 1:
                    sums[0] += mask * vb
                    sums[1] += mask * (va + vb)
                    sums[2] += mask * (va * va + vb * vb)
                else:
                    differ = result_ref[index * rows + at : index * rows + at + block_rows] - va
                    masked = mask * differ
                    sums[0] += masked
                    sums[1] += masked * differ
                    sums[2] += masked * vb
            lines = [total(value) for value in sums]
            if unit == 1:
                base_sums(window, lines)
            else:
                store(unit - 2, window, lines)


def line_at(groups, group, window, kind):
    return (window * 3 + kind) * groups + group


def pass_kernel(given_ref, out_ref):
    pass


def early_kernel(
    front, own_ref, scale_ref, one_ref, two_ref, three_ref, cols_ref, ends_ref, out_ref, picks_ref, masks_ref,
    pre_ref, first_ref, second_ref, result_ref, base_ref,
):
    windows, block_rows, width = own_ref.shape[1:]
    groups = picks_ref.shape[0]
    outputs = three_ref.shape[1]
    device = lax.axis_index("rows")
    place = lax.rem(device, front)
    corner = device // front
    total_groups = cols_ref.shape[1]
    line_ids = lax.broadcasted_iota(jnp.int32, (groups, total_groups), 0)
    spot_ids = lax.broadcasted_iota(jnp.int32, (groups, total_groups), 1)
    mine = jnp.where(spot_ids == line_ids + place * groups, cols_ref[...].astype(jnp.float32), 0.0)
    wanted = jnp.sum(mine, axis=1, keepdims=True).astype(jnp.int32)
    lane_ids = lax.broadcasted_iota(jnp.int32, (groups, width), 1)
    picks_ref[...] = jnp.where(lane_ids == wanted, 1.0, 0.0).astype(jnp.bfloat16)
    sublane = lax.broadcasted_iota(jnp.int32, (block_rows, outputs), 0)
    ends = [jnp.broadcast_to(ends_ref[0:1, window : window + 1], (block_rows, outputs)) for window in range(windows)]
    for peer in range(front):
        first_row = (corner * front + member_of(place, peer, front)) * block_rows
        for window in range(windows):
            masks_ref[peer, window] = jnp.where(sublane + first_row < ends[window], 1.0, 0.0)
    counts = []
    for window in range(windows):
        counts.append(ends[window][0:1].astype(jnp.float32) + (counts[-1] if counts else 0.0))

    def base_sums(window, lines):
        lines = lines + [counts[window]]
        start = 3 * windows * groups + 4 * window
        out_ref[start : start + 4, :] = jnp.concatenate(lines, 0)

    def store(group, window, lines):
        for kind in range(3):
            at = line_at(groups, group, window, kind)
            out_ref[at : at + 1, :] = lines[kind]

    rows = windows * block_rows
    units = range(groups + 2)
    delta, picked = prepare([own_ref], scale_ref[...], picks_ref[...], one_ref, pre_ref)
    fill(units, rows, pre_ref, delta, picked, first_ref)
    result_ref[...] = tail(first_ref, second_ref, two_ref, three_ref)
    tally(
        units, 1, windows, block_rows, lambda peer, window: masks_ref[0, window], result_ref, base_ref, base_sums, store
    )


def late_kernel(front, chunks, *refs):
    pieces = refs[: front - 1]
    (scale_ref, one_ref, two_ref, three_ref, picks_ref, masks_ref, early_ref, out_ref) = refs[front - 1 : front + 7]
    (pre_ref, first_ref, second_ref, result_ref, base_ref) = refs[front + 7 :]
    windows, block_rows = pieces[0].shape[1:3]
    groups = picks_ref.shape[0]
    rows = (front - 1) * windows * block_rows
    stats = 3 * windows * groups

    def mask_of(peer, window):
        return masks_ref[peer + 1, window]

    def base_sums(window, lines):
        at = stats + 4 * window
        out_ref[at : at + 3, :] = early_ref[at : at + 3, :] + jnp.concatenate(lines, 0)
        out_ref[at + 3 : at + 4, :] = early_ref[at + 3 : at + 4, :]

    def store(group, window, lines):
        for kind in range(3):
            at = line_at(groups, group, window, kind)
            out_ref[at : at + 1, :] = early_ref[at : at + 1, :] + lines[kind]

    delta, picked = prepare(list(pieces), scale_ref[...], picks_ref[...], one_ref, pre_ref)
    fill(chunks[0], rows, pre_ref, delta, picked, first_ref.at[0])
    for index, units in enumerate(chunks):
        slot = index % 2
        if index + 1 < len(chunks):
            fill(chunks[index + 1], rows, pre_ref, delta, picked, first_ref.at[1 - slot])
        result_ref[slot] = tail(first_ref.at[slot], second_ref.at[slot], two_ref, three_ref)
        tally(units, front - 1, windows, block_rows, mask_of, result_ref.at[slot], base_ref, base_sums, store)


def conclude_kernel(own_ref, other_ref, out_ref, variance_ref):
    windows, groups = out_ref.shape[1:3]
    stats = 3 * windows * groups
    running = None
    for window in range(windows):
        at = stats + 4 * window
        pieces = [own_ref[at : at + 3] + other_ref[at : at + 3]]
        for kind in range(3):
            line = line_at(groups, 0, window, kind)
            pieces.append(own_ref[line : line + groups] + other_ref[line : line + groups])
        running = pieces if running is None else [former + latter for former, latter in zip(running, pieces)]
        share = 1.0 / own_ref[at + 3 : at + 4]
        base, sum_d, squares_d, cross = running
        mean = base[1:2] * (0.5 * share)
        variance = (base[2:3] - base[1:2] * mean) * (0.5 * share)
        weight = share / variance
        out_ref[0, window] = (cross - (base[0:1] * share) * sum_d) * weight
        out_ref[1, window] = squares_d * (0.5 * weight)
        variance_ref[window : window + 1, :] = variance


def assemble_kernel(front, own_ref, *refs):
    peers = refs[: front - 1]
    settled_ref, first_ref, total_ref, variance_ref = refs[front - 1 :]
    place = lax.rem(lax.axis_index("rows"), front)
    groups = own_ref.shape[2]
    for peer, ref in enumerate([own_ref] + list(peers)):
        start = pl.multiple_of(member_of(place, peer, front) * groups, groups)
        first_ref[:, pl.ds(start, groups), :] = ref[0]
        total_ref[:, pl.ds(start, groups), :] = ref[1]
    variance_ref[...] = settled_ref[...]


def near(values):
    return pltpu.with_memory_space_constraint(values, pltpu.VMEM)


def exchange(values, pairs):
    return lax.ppermute(values, "rows", pairs)


def local(base_a, base_b, input_scale, layer_one, layer_two, layer_three, swap_cols, window_ends):
    windows, block_rows, width = base_a.shape
    size = lax.axis_size("rows")
    total_groups = swap_cols.shape[0]
    hidden = layer_one.shape[1]
    outputs = layer_three.shape[1]
    back = 2 if size % 2 == 0 else 1
    front = size // back
    groups = total_groups // front
    late_rows = (front - 1) * windows * block_rows
    per_chunk = units_per_chunk(groups + 2, late_rows)
    chunks = [range(at, at + per_chunk) for at in range(0, groups + 2, per_chunk)]
    height = (3 * groups + 4) * windows

    def pairs_of(peer):
        pairs = []
        for device in range(size):
            corner, place = divmod(device, front)
            source = (place ^ peer) if front & (front - 1) == 0 else (place + peer) % front
            pairs.append((corner * front + source, device))
        return pairs

    vmem = pl.BlockSpec(memory_space=pltpu.VMEM)

    def room_of(spaces):
        held = sum(math.prod(space.shape) * jnp.dtype(space.dtype).itemsize for space in spaces)
        return pltpu.CompilerParams(vmem_limit_bytes=held + SPARE_BYTES)

    def work_of(rows):
        return pl.CostEstimate(
            flops=2 * rows * hidden * (hidden + outputs),
            transcendentals=2 * rows * hidden,
            bytes_accessed=2 * (layer_one.size + layer_two.size + layer_three.size),
        )

    own = jnp.stack([base_a, base_b]).astype(jnp.float32)
    own = pl.pallas_call(
        pass_kernel,
        out_shape=pltpu.VMEM(own.shape, own.dtype),
        in_specs=[pl.BlockSpec(memory_space=pltpu.VMEM)],
        out_specs=pl.BlockSpec(memory_space=pltpu.VMEM),
        input_output_aliases={0: 0},
        cost_estimate=pl.CostEstimate(flops=PASS_FLOPS, transcendentals=0, bytes_accessed=0),
        compiler_params=pltpu.CompilerParams(vmem_limit_bytes=1024 * 1024),
        name="pass",
    )(near(own))
    own = near(own)
    received = [exchange(own, pairs_of(peer)) for peer in range(1, front)]
    scale = input_scale.reshape(1, width)
    scales, one, two, three = near(scale), near(layer_one), near(layer_two), near(layer_three)

    def early(*args):
        return early_kernel(front, *args)

    own_rows = windows * block_rows
    early_rows = (groups + 2) * own_rows
    early_scratch = [
        pltpu.VMEM((2 * own_rows, hidden), jnp.float32),
        pltpu.VMEM((early_rows, hidden), jnp.bfloat16),
        pltpu.VMEM((early_rows, hidden), jnp.bfloat16),
        pltpu.VMEM((early_rows, outputs), jnp.float32),
        pltpu.VMEM((2, own_rows, outputs), jnp.float32),
    ]
    sums, picks, masks = pl.pallas_call(
        early,
        out_shape=(
            pltpu.VMEM((height, outputs), jnp.float32),
            pltpu.VMEM((groups, width), jnp.bfloat16),
            pltpu.VMEM((front, windows, block_rows, outputs), jnp.float32),
        ),
        in_specs=[vmem] * 7,
        out_specs=(vmem,) * 3,
        scratch_shapes=early_scratch,
        cost_estimate=work_of(early_rows),
        compiler_params=room_of(early_scratch),
        name="early",
    )(
        own,
        scales,
        one,
        two,
        three,
        near(swap_cols.reshape(1, total_groups)),
        near(window_ends.reshape(1, windows)),
    )

    def late(*args):
        return late_kernel(front, chunks, *args)

    chunk_rows = per_chunk * late_rows
    late_scratch = [
        pltpu.VMEM((2 * late_rows, hidden), jnp.float32),
        pltpu.VMEM((2, chunk_rows, hidden), jnp.bfloat16),
        pltpu.VMEM((2, chunk_rows, hidden), jnp.bfloat16),
        pltpu.VMEM((2, chunk_rows, outputs), jnp.float32),
        pltpu.VMEM((2, late_rows, outputs), jnp.float32),
    ]
    partial = pl.pallas_call(
        late,
        out_shape=pltpu.VMEM((height, outputs), jnp.float32),
        in_specs=[vmem] * (front + 6),
        out_specs=vmem,
        scratch_shapes=late_scratch,
        cost_estimate=work_of(len(chunks) * chunk_rows),
        compiler_params=room_of(late_scratch),
        name="late",
    )(*(near(value) for value in (*received, scales, one, two, three, picks, masks, sums)))
    partial = near(partial)
    if back == 1:
        other = jnp.zeros_like(partial)
    else:
        other = exchange(partial, [(device, (device + front) % size) for device in range(size)])

    settled, variance = pl.pallas_call(
        conclude_kernel,
        out_shape=(
            pltpu.VMEM((2, windows, groups, outputs), jnp.float32),
            pltpu.VMEM((windows, outputs), jnp.float32),
        ),
        in_specs=[vmem, vmem],
        out_specs=(vmem, vmem),
        compiler_params=pltpu.CompilerParams(vmem_limit_bytes=SPARE_BYTES),
        name="conclude",
    )(partial, near(other))

    gathered = [exchange(settled, pairs_of(peer)) for peer in range(1, front)]

    def assemble(*args):
        return assemble_kernel(front, *args)

    whole = jax.ShapeDtypeStruct((windows, total_groups, outputs), jnp.float32)
    return pl.pallas_call(
        assemble,
        out_shape=(whole, whole, jax.ShapeDtypeStruct((windows, outputs), jnp.float32)),
        in_specs=[vmem] * (front + 1),
        out_specs=(vmem, vmem, vmem),
        compiler_params=pltpu.CompilerParams(vmem_limit_bytes=SPARE_BYTES),
        name="assemble",
    )(*(near(value) for value in (settled, *gathered, variance)))


def solution(mesh):
    in_specs = (P(None, "rows", None), P(None, "rows", None), P(), P(), P(), P(), P("par"), P())
    out_specs = (P(None, "par", None), P(None, "par", None), P())
    return jax.shard_map(local, mesh=mesh, in_specs=in_specs, out_specs=out_specs, check_vma=False)
```

time: 31.9 us -> 30.8 us (0.966)
  Pallas kernels: 10.5 us -> 9.09 us
  waiting for transfers between devices: 7.9 us -> 8.96 us
  starting transfers between devices: 11.8 us -> 10.9 us
    pallas_call x3 -> x4, Pallas kernels: 9.77 us -> 8.37 us  [the longest x1 5.91 us: local(): pl.pallas_call(late, out_shape=pltpu.VMEM((height, outputs), jnp.float32)...]
    ppermute x7, waiting for transfers between devices: 7.9 us -> 8.96 us  [exchange(): return lax.ppermute(values, 'rows', pairs)]
    ppermute x7, starting transfers between devices: 11.8 us -> 10.9 us  [exchange(): return lax.ppermute(values, 'rows', pairs)]
  transfers between devices with their start and end apart: 7 -> 7, of which waited for: 4 -> 6; matrix products, arithmetic and copies ran while one was open for 0% -> 0% of each run, Pallas kernels for 12% -> 8%
where the time goes in v3:
time: 30.8 us; the launch traced here: 30.5 us
  starting transfers between devices  10.9 us (35%)
  Pallas kernels  9.09 us (30%)
  waiting for transfers between devices  8.96 us (29%)
  other arithmetic  0.74 us (2%)
  between operations  0.73 us (2%)
    ppermute x7, starting transfers between devices, exchange(): return lax.ppermute(values, 'rows', pairs)  10.9 us
    ppermute x7, waiting for transfers between devices, exchange(): return lax.ppermute(values, 'rows', pairs)  8.96 us
    pallas_call x1, Pallas kernels, local(): pl.pallas_call(late, out_shape=pltpu.VMEM((height, outputs), jnp.float32)...  5.91 us
    pallas_call x1, Pallas kernels, local(): pl.pallas_call(early, out_shape=(pltpu.VMEM((height, outputs), jnp.float3...  2.42 us
    convert_element_type x1, other arithmetic, local(): own = jnp.stack([base_a, base_b]).astype(jnp.float32)  0.74 us
    pallas_call x1, Pallas kernels, local(): pl.pallas_call(assemble, out_shape=(whole, whole, jax.ShapeDtypeStruct((w...  0.72 us
  transfers between devices with their start and end apart: 7, of which 6 were waited for; matrix products, arithmetic and copies ran while one was open for 0% of the time, Pallas kernels for 8%

profile of v3, /device:TPU:0, one launch (start us, length us, event | category | flops | bytes accessed | tf_op | source)
XLA Modules:
  0.0 30.5 jit_solution(4435771071705116794)
XLA Ops:
  0.6 0.7 %maximum_convert_fusion.given_ref = f32[2,4,8,256]{3,2,1,0:T(8,128)S(1)} fusion(bf16[1,4,8,256]{3,2,1,0:T(8,128)(2,1)} %bitcast.9, bf16[1,4,8,256]{3,2,1,0:T(8,128)(2,1)} %bitcast.10), kind=kLoop, calls=%fused_computation | loop fusion | flops 32768 | bytes 98304 | tf_op jit(solution)/shard_map/convert_element_type | solution.py:277
  1.4 0.0 copy-start
  1.4 0.0 copy-start.1
  1.4 0.0 copy-start.2
  1.4 0.0 copy-start.3
  1.4 0.0 copy-start.4
  1.4 0.0 copy-start.5
  1.4 4.1 %collective-permute-start.2 = (f32[2,4,8,256]{3,2,1,0:T(8,128)S(1)}, f32[2,4,8,256]{3,2,1,0:T(8,128)S(1)}, u32[]{:S(2)}, u32[]{:S(2)}) collective-permute-start(f32[2,4,8,256]{3,2,1,0:T(8,128)S(1)} %pass.1.args_0_), channel_id=1, source_target_pairs={{12,0},{8,4},{4,8},{0,12},{28,16},{24,20},{20,24},{16,28},{13,1},{... | collective-permute-start | bytes 196616 | tf_op jit(solution)/shard_map/ppermute | solution.py:239
  5.5 0.4 %collective-permute-start.1 = (f32[2,4,8,256]{3,2,1,0:T(8,128)S(1)}, f32[2,4,8,256]{3,2,1,0:T(8,128)S(1)}, u32[]{:S(2)}, u32[]{:S(2)}) collective-permute-start(f32[2,4,8,256]{3,2,1,0:T(8,128)S(1)} %pass.1.args_0_), channel_id=1, source_target_pairs={{8,0},{12,4},{0,8},{4,12},{24,16},{28,20},{16,24},{20,28},{9,1},{1... | collective-permute-start | bytes 196616 | tf_op jit(solution)/shard_map/ppermute | solution.py:239
  6.0 0.2 collective-permute-start
  6.2 0.0 copy-done
  6.2 0.0 copy-done.1
  6.2 0.0 copy-done.2
  6.2 0.0 copy-done.3
  6.2 0.0 copy-done.4
  6.2 0.0 copy-done.5
  6.2 2.4 %early.1 = (f32[208,128]{1,0:T(8,128)S(1)}, bf16[16,256]{1,0:T(8,128)(2,1)S(1)}, f32[4,4,8,128]{3,2,1,0:T(8,128)S(1)}) custom-call(f32[2,4,8,256]{3,2,1,0:T(8,128)S(1)} %pass.1.args_0_, f32[1,256]{1,0:T(1,128)S(1)} %bitcast.5, bf16[256,1024]{1,0:T(8,128)(2,1)S(1)} %copy-done.1, bf16[1024,1024]{1,0:T(8,128)(2,1)S(1)} %copy-done, ...), custom_call_target="tpu_custom_call" | custom-call | flops 1358954496 | bytes 2883584 | tf_op jit(solution)/shard_map/early/pallas_call | solution.py:305
  8.6 0.0 collective-permute-done.2.args_2_
  8.6 1.2 %collective-permute-done.1.args_1_ = f32[2,4,8,256]{3,2,1,0:T(8,128)S(1)} collective-permute-done((f32[2,4,8,256]{3,2,1,0:T(8,128)S(1)}, f32[2,4,8,256]{3,2,1,0:T(8,128)S(1)}, u32[]{:S(2)}, u32[]{:S(2)}) %collective-permute-start.1) | collective-permute-done | bytes 65568 | tf_op jit(solution)/shard_map/ppermute | solution.py:239
  9.8 0.4 %collective-permute-done.args_0_ = f32[2,4,8,256]{3,2,1,0:T(8,128)S(1)} collective-permute-done((f32[2,4,8,256]{3,2,1,0:T(8,128)S(1)}, f32[2,4,8,256]{3,2,1,0:T(8,128)S(1)}, u32[]{:S(2)}, u32[]{:S(2)}) %collective-permute-start) | collective-permute-done | bytes 65568 | tf_op jit(solution)/shard_map/ppermute | solution.py:239
  10.2 5.9 %late.1.own_ref = f32[208,128]{1,0:T(8,128)S(1)} custom-call(f32[2,4,8,256]{3,2,1,0:T(8,128)S(1)} %collective-permute-done.args_0_, f32[2,4,8,256]{3,2,1,0:T(8,128)S(1)} %collective-permute-done.1.args_1_, f32[2,4,8,256]{3,2,1,0:T(8,128)S(1)} %collective-permute-done.2.args_2_, f32[1,256]{1,0:T(1,128)S(1)} %bitcast.6, bf16[256,1024]{1,0:T(8,128)(2,1)S(1)} %copy-done.1, ...), custom_call_target="tpu_custom_call" | custom-call | flops 4076863488 | bytes 2883584 | tf_op jit(solution)/shard_map/late/pallas_call | solution.py:339
  16.2 2.7 %collective-permute-start.3 = (f32[208,128]{1,0:T(8,128)S(1)}, f32[208,128]{1,0:T(8,128)S(1)}, u32[]{:S(2)}, u32[]{:S(2)}) collective-permute-start(f32[208,128]{1,0:T(8,128)S(1)} %late.1.own_ref), channel_id=1, source_target_pairs={{0,16},{4,20},{8,24},{12,28},{16,0},{20,4},{24,8},{28,12},{1,17},{... | collective-permute-start | bytes 319496 | tf_op jit(solution)/shard_map/ppermute | solution.py:239
  18.8 4.3 %collective-permute-done.3.other_ref = f32[208,128]{1,0:T(8,128)S(1)} collective-permute-done((f32[208,128]{1,0:T(8,128)S(1)}, f32[208,128]{1,0:T(8,128)S(1)}, u32[]{:S(2)}, u32[]{:S(2)}) %collective-permute-start.3) | collective-permute-done | bytes 106528 | tf_op jit(solution)/shard_map/ppermute | solution.py:239
  23.1 0.9 %collective-permute-start.6 = (f32[2,4,16,128]{3,2,1,0:T(8,128)S(1)}, f32[2,4,16,128]{3,2,1,0:T(8,128)S(1)}, u32[]{:S(2)}, u32[]{:S(2)}) collective-permute-start(f32[2,4,16,128]{3,2,1,0:T(8,128)S(1)} %get-tuple-element.11.args_0_), channel_id=1, source_target_pairs={{12,0},{8,4},{4,8},{0,12},{28,16},{24,20},{20,24},{16,28},{13,1},{... | collective-permute-start | bytes 196616 | tf_op jit(solution)/shard_map/ppermute | solution.py:239
  24.0 1.5 %collective-permute-start.5 = (f32[2,4,16,128]{3,2,1,0:T(8,128)S(1)}, f32[2,4,16,128]{3,2,1,0:T(8,128)S(1)}, u32[]{:S(2)}, u32[]{:S(2)}) collective-permute-start(f32[2,4,16,128]{3,2,1,0:T(8,128)S(1)} %get-tuple-element.11.args_0_), channel_id=1, source_target_pairs={{8,0},{12,4},{0,8},{4,12},{24,16},{28,20},{16,24},{20,28},{9,1},{1... | collective-permute-start | bytes 196616 | tf_op jit(solution)/shard_map/ppermute | solution.py:239
  25.5 1.2 %collective-permute-start.4 = (f32[2,4,16,128]{3,2,1,0:T(8,128)S(1)}, f32[2,4,16,128]{3,2,1,0:T(8,128)S(1)}, u32[]{:S(2)}, u32[]{:S(2)}) collective-permute-start(f32[2,4,16,128]{3,2,1,0:T(8,128)S(1)} %get-tuple-element.11.args_0_), channel_id=1, source_target_pairs={{4,0},{0,4},{12,8},{8,12},{20,16},{16,20},{28,24},{24,28},{5,1},{1... | collective-permute-start | bytes 196616 | tf_op jit(solution)/shard_map/ppermute | solution.py:239
  26.7 1.7 %collective-permute-done.6.args_3_ = f32[2,4,16,128]{3,2,1,0:T(8,128)S(1)} collective-permute-done((f32[2,4,16,128]{3,2,1,0:T(8,128)S(1)}, f32[2,4,16,128]{3,2,1,0:T(8,128)S(1)}, u32[]{:S(2)}, u32[]{:S(2)}) %collective-permute-start.6) | collective-permute-done | bytes 65568 | tf_op jit(solution)/shard_map/ppermute | solution.py:239
  28.3 0.1 collective-permute-done.5.args_2_
  28.4 1.3 %collective-permute-done.4.args_1_ = f32[2,4,16,128]{3,2,1,0:T(8,128)S(1)} collective-permute-done((f32[2,4,16,128]{3,2,1,0:T(8,128)S(1)}, f32[2,4,16,128]{3,2,1,0:T(8,128)S(1)}, u32[]{:S(2)}, u32[]{:S(2)}) %collective-permute-start.4) | collective-permute-done | bytes 65568 | tf_op jit(solution)/shard_map/ppermute | solution.py:239
  29.8 0.7 %assemble.1 = (f32[4,64,128]{2,1,0:T(8,128)}, f32[4,64,128]{2,1,0:T(8,128)}, f32[4,128]{1,0:T(4,128)}) custom-call(f32[2,4,16,128]{3,2,1,0:T(8,128)S(1)} %get-tuple-element.11.args_0_, f32[2,4,16,128]{3,2,1,0:T(8,128)S(1)} %collective-permute-done.4.args_1_, f32[2,4,16,128]{3,2,1,0:T(8,128)S(1)} %collective-permute-done.5.args_2_, ...), custom_call_target="tpu_custom_call" | custom-call | tf_op jit(solution)/shard_map/assemble/pallas_call | solution.py:373
  (2 shorter events, 0.0 us)
Async XLA Ops:
  1.4 4.8 %copy-start = (bf16[1024,1024]{1,0:T(8,128)(2,1)S(1)}, bf16[1024,1024]{1,0:T(8,128)(2,1)}, u32[]{:S(2)}) copy-start(bf16[1024,1024]{1,0:T(8,128)(2,1)} %args_5_.4) | copy-start | bytes 6291460
  1.4 4.8 %copy-start.1 = (bf16[256,1024]{1,0:T(8,128)(2,1)S(1)}, bf16[256,1024]{1,0:T(8,128)(2,1)}, u32[]{:S(2)}) copy-start(bf16[256,1024]{1,0:T(8,128)(2,1)} %args_4_.6) | copy-start | bytes 1572868
  1.4 4.8 %copy-start.2 = (bf16[1024,128]{1,0:T(8,128)(2,1)S(1)}, bf16[1024,128]{1,0:T(8,128)(2,1)}, u32[]{:S(2)}) copy-start(bf16[1024,128]{1,0:T(8,128)(2,1)} %args_6_.4) | copy-start | bytes 786436
  1.4 4.8 %copy-start.3 = (f32[256]{0:T(256)S(1)}, f32[256]{0:T(256)}, u32[]{:S(2)}) copy-start(f32[256]{0:T(256)} %param.10) | copy-start | bytes 3076
  1.4 4.8 %copy-start.4 = (s32[64]{0:T(128)S(1)}, s32[64]{0:T(128)}, u32[]{:S(2)}) copy-start(s32[64]{0:T(128)} %param.14) | copy-start | bytes 772
  1.4 4.8 %copy-start.5 = (s32[4]{0:T(128)S(1)}, s32[4]{0:T(128)}, u32[]{:S(2)}) copy-start(s32[4]{0:T(128)} %param.15) | copy-start | bytes 52
  1.4 7.2 %collective-permute-start.2 = (f32[2,4,8,256]{3,2,1,0:T(8,128)S(1)}, f32[2,4,8,256]{3,2,1,0:T(8,128)S(1)}, u32[]{:S(2)}, u32[]{:S(2)}) collective-permute-start(f32[2,4,8,256]{3,2,1,0:T(8,128)S(1)} %pass.1.args_0_), channel_id=1, source_target_pairs={{12,0},{8,4},{4,8},{0,12},{28,16},{24,20},{20,24},{16,28},{13,1},{... | collective-permute-start | bytes 196616 | tf_op jit(solution)/shard_map/ppermute | solution.py:239
  5.5 4.3 %collective-permute-start.1 = (f32[2,4,8,256]{3,2,1,0:T(8,128)S(1)}, f32[2,4,8,256]{3,2,1,0:T(8,128)S(1)}, u32[]{:S(2)}, u32[]{:S(2)}) collective-permute-start(f32[2,4,8,256]{3,2,1,0:T(8,128)S(1)} %pass.1.args_0_), channel_id=1, source_target_pairs={{8,0},{12,4},{0,8},{4,12},{24,16},{28,20},{16,24},{20,28},{9,1},{1... | collective-permute-start | bytes 196616 | tf_op jit(solution)/shard_map/ppermute | solution.py:239
  6.0 4.3 %collective-permute-start = (f32[2,4,8,256]{3,2,1,0:T(8,128)S(1)}, f32[2,4,8,256]{3,2,1,0:T(8,128)S(1)}, u32[]{:S(2)}, u32[]{:S(2)}) collective-permute-start(f32[2,4,8,256]{3,2,1,0:T(8,128)S(1)} %pass.1.args_0_), channel_id=1, source_target_pairs={{4,0},{0,4},{12,8},{8,12},{20,16},{16,20},{28,24},{24,28},{5,1},{1... | collective-permute-start | bytes 196616 | tf_op jit(solution)/shard_map/ppermute | solution.py:239
  16.2 6.9 %collective-permute-start.3 = (f32[208,128]{1,0:T(8,128)S(1)}, f32[208,128]{1,0:T(8,128)S(1)}, u32[]{:S(2)}, u32[]{:S(2)}) collective-permute-start(f32[208,128]{1,0:T(8,128)S(1)} %late.1.own_ref), channel_id=1, source_target_pairs={{0,16},{4,20},{8,24},{12,28},{16,0},{20,4},{24,8},{28,12},{1,17},{... | collective-permute-start | bytes 319496 | tf_op jit(solution)/shard_map/ppermute | solution.py:239
  23.1 5.2 %collective-permute-start.6 = (f32[2,4,16,128]{3,2,1,0:T(8,128)S(1)}, f32[2,4,16,128]{3,2,1,0:T(8,128)S(1)}, u32[]{:S(2)}, u32[]{:S(2)}) collective-permute-start(f32[2,4,16,128]{3,2,1,0:T(8,128)S(1)} %get-tuple-element.11.args_0_), channel_id=1, source_target_pairs={{12,0},{8,4},{4,8},{0,12},{28,16},{24,20},{20,24},{16,28},{13,1},{... | collective-permute-start | bytes 196616 | tf_op jit(solution)/shard_map/ppermute | solution.py:239
  24.0 4.4 %collective-permute-start.5 = (f32[2,4,16,128]{3,2,1,0:T(8,128)S(1)}, f32[2,4,16,128]{3,2,1,0:T(8,128)S(1)}, u32[]{:S(2)}, u32[]{:S(2)}) collective-permute-start(f32[2,4,16,128]{3,2,1,0:T(8,128)S(1)} %get-tuple-element.11.args_0_), channel_id=1, source_target_pairs={{8,0},{12,4},{0,8},{4,12},{24,16},{28,20},{16,24},{20,28},{9,1},{1... | collective-permute-start | bytes 196616 | tf_op jit(solution)/shard_map/ppermute | solution.py:239
  25.5 4.3 %collective-permute-start.4 = (f32[2,4,16,128]{3,2,1,0:T(8,128)S(1)}, f32[2,4,16,128]{3,2,1,0:T(8,128)S(1)}, u32[]{:S(2)}, u32[]{:S(2)}) collective-permute-start(f32[2,4,16,128]{3,2,1,0:T(8,128)S(1)} %get-tuple-element.11.args_0_), channel_id=1, source_target_pairs={{4,0},{0,4},{12,8},{8,12},{20,16},{16,20},{28,24},{24,28},{5,1},{1... | collective-permute-start | bytes 196616 | tf_op jit(solution)/shard_map/ppermute | solution.py:239

commit v4 on v3

--- a/solution.py
+++ b/solution.py
@@ -23,6 +23,11 @@
 
 def units_per_chunk(units, rows):
     return max(count for count in range(1, units + 1) if units % count == 0 and (count == 1 or count * rows <= CHUNK_ROWS))
+
+
+def order_of(front):
+    peers = list(range(1, front))
+    return peers[1:2] + peers[:1] + peers[2:]
 
 
 def member_of(place, peer, front):
@@ -174,9 +179,10 @@
     groups = picks_ref.shape[0]
     rows = (front - 1) * windows * block_rows
     stats = 3 * windows * groups
+    order = order_of(front)
 
     def mask_of(peer, window):
-        return masks_ref[peer + 1, window]
+        return masks_ref[order[peer], window]
 
     def base_sums(window, lines):
         at = stats + 4 * window
@@ -224,7 +230,7 @@
     settled_ref, first_ref, total_ref, variance_ref = refs[front - 1 :]
     place = lax.rem(lax.axis_index("rows"), front)
     groups = own_ref.shape[2]
-    for peer, ref in enumerate([own_ref] + list(peers)):
+    for peer, ref in zip([0, *order_of(front)], [own_ref] + list(peers)):
         start = pl.multiple_of(member_of(place, peer, front) * groups, groups)
         first_ref[:, pl.ds(start, groups), :] = ref[0]
         total_ref[:, pl.ds(start, groups), :] = ref[1]
@@ -252,6 +258,7 @@
     per_chunk = units_per_chunk(groups + 2, late_rows)
     chunks = [range(at, at + per_chunk) for at in range(0, groups + 2, per_chunk)]
     height = (3 * groups + 4) * windows
+    order = order_of(front)
 
     def pairs_of(peer):
         pairs = []
@@ -286,7 +293,7 @@
         name="pass",
     )(near(own))
     own = near(own)
-    received = [exchange(own, pairs_of(peer)) for peer in range(1, front)]
+    received = [exchange(own, pairs_of(peer)) for peer in order]
     scale = input_scale.reshape(1, width)
     scales, one, two, three = near(scale), near(layer_one), near(layer_two), near(layer_three)
 
@@ -364,7 +371,7 @@
         name="conclude",
     )(partial, near(other))
 
-    gathered = [exchange(settled, pairs_of(peer)) for peer in range(1, front)]
+    gathered = [exchange(settled, pairs_of(peer)) for peer in order]
 
     def assemble(*args):
         return assemble_kernel(front, *args)

time: 30.8 us -> 30.3 us (0.984)
  waiting for transfers between devices: 8.96 us -> 8.48 us
    ppermute x7, waiting for transfers between devices: 8.96 us -> 8.48 us  [exchange(): return lax.ppermute(values, 'rows', pairs)]
where the time goes in v4:
time: 30.3 us; the launch traced here: 30 us
  starting transfers between devices  10.9 us (36%)
  Pallas kernels  9.09 us (30%)
  waiting for transfers between devices  8.48 us (28%)
  other arithmetic  0.74 us (2%)
  between operations  0.73 us (2%)
    ppermute x7, starting transfers between devices, exchange(): return lax.ppermute(values, 'rows', pairs)  10.9 us
    ppermute x7, waiting for transfers between devices, exchange(): return lax.ppermute(values, 'rows', pairs)  8.48 us
    pallas_call x1, Pallas kernels, local(): pl.pallas_call(late, out_shape=pltpu.VMEM((height, outputs), jnp.float32)...  5.91 us
    pallas_call x1, Pallas kernels, local(): pl.pallas_call(early, out_shape=(pltpu.VMEM((height, outputs), jnp.float3...  2.42 us
    convert_element_type x1, other arithmetic, local(): own = jnp.stack([base_a, base_b]).astype(jnp.float32)  0.74 us
    pallas_call x1, Pallas kernels, local(): pl.pallas_call(assemble, out_shape=(whole, whole, jax.ShapeDtypeStruct((w...  0.72 us
  transfers between devices with their start and end apart: 7, of which 6 were waited for; matrix products, arithmetic and copies ran while one was open for 0% of the time, Pallas kernels for 8%

profile of v4, /device:TPU:0, one launch (start us, length us, event | category | flops | bytes accessed | tf_op | source)
XLA Modules:
  0.0 30.0 jit_solution(16967405104855759101)
XLA Ops:
  0.6 0.7 %maximum_convert_fusion.given_ref = f32[2,4,8,256]{3,2,1,0:T(8,128)S(1)} fusion(bf16[1,4,8,256]{3,2,1,0:T(8,128)(2,1)} %bitcast.9, bf16[1,4,8,256]{3,2,1,0:T(8,128)(2,1)} %bitcast.10), kind=kLoop, calls=%fused_computation | loop fusion | flops 32768 | bytes 98304 | tf_op jit(solution)/shard_map/convert_element_type | solution.py:284
  1.4 0.0 copy-start
  1.4 0.0 copy-start.1
  1.4 0.0 copy-start.2
  1.4 0.0 copy-start.3
  1.4 0.0 copy-start.4
  1.4 0.0 copy-start.5
  1.4 4.1 %collective-permute-start.2 = (f32[2,4,8,256]{3,2,1,0:T(8,128)S(1)}, f32[2,4,8,256]{3,2,1,0:T(8,128)S(1)}, u32[]{:S(2)}, u32[]{:S(2)}) collective-permute-start(f32[2,4,8,256]{3,2,1,0:T(8,128)S(1)} %pass.1.args_0_), channel_id=1, source_target_pairs={{12,0},{8,4},{4,8},{0,12},{28,16},{24,20},{20,24},{16,28},{13,1},{... | collective-permute-start | bytes 196616 | tf_op jit(solution)/shard_map/ppermute | solution.py:245
  5.5 0.5 %collective-permute-start.1 = (f32[2,4,8,256]{3,2,1,0:T(8,128)S(1)}, f32[2,4,8,256]{3,2,1,0:T(8,128)S(1)}, u32[]{:S(2)}, u32[]{:S(2)}) collective-permute-start(f32[2,4,8,256]{3,2,1,0:T(8,128)S(1)} %pass.1.args_0_), channel_id=1, source_target_pairs={{4,0},{0,4},{12,8},{8,12},{20,16},{16,20},{28,24},{24,28},{5,1},{1... | collective-permute-start | bytes 196616 | tf_op jit(solution)/shard_map/ppermute | solution.py:245
  6.0 0.1 collective-permute-start
  6.2 0.0 copy-done
  6.2 0.0 copy-done.1
  6.2 0.0 copy-done.2
  6.2 0.0 copy-done.3
  6.2 0.0 copy-done.4
  6.2 0.0 copy-done.5
  6.2 2.4 %early.1 = (f32[208,128]{1,0:T(8,128)S(1)}, bf16[16,256]{1,0:T(8,128)(2,1)S(1)}, f32[4,4,8,128]{3,2,1,0:T(8,128)S(1)}) custom-call(f32[2,4,8,256]{3,2,1,0:T(8,128)S(1)} %pass.1.args_0_, f32[1,256]{1,0:T(1,128)S(1)} %bitcast.5, bf16[256,1024]{1,0:T(8,128)(2,1)S(1)} %copy-done.1, bf16[1024,1024]{1,0:T(8,128)(2,1)S(1)} %copy-done, ...), custom_call_target="tpu_custom_call" | custom-call | flops 1358954496 | bytes 2883584 | tf_op jit(solution)/shard_map/early/pallas_call | solution.py:312
  8.6 0.0 collective-permute-done.2.args_2_
  8.6 1.2 %collective-permute-done.1.args_1_ = f32[2,4,8,256]{3,2,1,0:T(8,128)S(1)} collective-permute-done((f32[2,4,8,256]{3,2,1,0:T(8,128)S(1)}, f32[2,4,8,256]{3,2,1,0:T(8,128)S(1)}, u32[]{:S(2)}, u32[]{:S(2)}) %collective-permute-start.1) | collective-permute-done | bytes 65568 | tf_op jit(solution)/shard_map/ppermute | solution.py:245
  9.8 0.5 %collective-permute-done.args_0_ = f32[2,4,8,256]{3,2,1,0:T(8,128)S(1)} collective-permute-done((f32[2,4,8,256]{3,2,1,0:T(8,128)S(1)}, f32[2,4,8,256]{3,2,1,0:T(8,128)S(1)}, u32[]{:S(2)}, u32[]{:S(2)}) %collective-permute-start) | collective-permute-done | bytes 65568 | tf_op jit(solution)/shard_map/ppermute | solution.py:245
  10.3 5.9 %late.1.own_ref = f32[208,128]{1,0:T(8,128)S(1)} custom-call(f32[2,4,8,256]{3,2,1,0:T(8,128)S(1)} %collective-permute-done.args_0_, f32[2,4,8,256]{3,2,1,0:T(8,128)S(1)} %collective-permute-done.1.args_1_, f32[2,4,8,256]{3,2,1,0:T(8,128)S(1)} %collective-permute-done.2.args_2_, f32[1,256]{1,0:T(1,128)S(1)} %bitcast.6, bf16[256,1024]{1,0:T(8,128)(2,1)S(1)} %copy-done.1, ...), custom_call_target="tpu_custom_call" | custom-call | flops 4076863488 | bytes 2883584 | tf_op jit(solution)/shard_map/late/pallas_call | solution.py:346
  16.2 2.7 %collective-permute-start.3 = (f32[208,128]{1,0:T(8,128)S(1)}, f32[208,128]{1,0:T(8,128)S(1)}, u32[]{:S(2)}, u32[]{:S(2)}) collective-permute-start(f32[208,128]{1,0:T(8,128)S(1)} %late.1.own_ref), channel_id=1, source_target_pairs={{0,16},{4,20},{8,24},{12,28},{16,0},{20,4},{24,8},{28,12},{1,17},{... | collective-permute-start | bytes 319496 | tf_op jit(solution)/shard_map/ppermute | solution.py:245
  18.9 4.1 %collective-permute-done.3.other_ref = f32[208,128]{1,0:T(8,128)S(1)} collective-permute-done((f32[208,128]{1,0:T(8,128)S(1)}, f32[208,128]{1,0:T(8,128)S(1)}, u32[]{:S(2)}, u32[]{:S(2)}) %collective-permute-start.3) | collective-permute-done | bytes 106528 | tf_op jit(solution)/shard_map/ppermute | solution.py:245
  23.0 1.0 %collective-permute-start.6 = (f32[2,4,16,128]{3,2,1,0:T(8,128)S(1)}, f32[2,4,16,128]{3,2,1,0:T(8,128)S(1)}, u32[]{:S(2)}, u32[]{:S(2)}) collective-permute-start(f32[2,4,16,128]{3,2,1,0:T(8,128)S(1)} %get-tuple-element.11.args_0_), channel_id=1, source_target_pairs={{12,0},{8,4},{4,8},{0,12},{28,16},{24,20},{20,24},{16,28},{13,1},{... | collective-permute-start | bytes 196616 | tf_op jit(solution)/shard_map/ppermute | solution.py:245
  23.9 1.1 %collective-permute-start.5 = (f32[2,4,16,128]{3,2,1,0:T(8,128)S(1)}, f32[2,4,16,128]{3,2,1,0:T(8,128)S(1)}, u32[]{:S(2)}, u32[]{:S(2)}) collective-permute-start(f32[2,4,16,128]{3,2,1,0:T(8,128)S(1)} %get-tuple-element.11.args_0_), channel_id=1, source_target_pairs={{4,0},{0,4},{12,8},{8,12},{20,16},{16,20},{28,24},{24,28},{5,1},{1... | collective-permute-start | bytes 196616 | tf_op jit(solution)/shard_map/ppermute | solution.py:245
  25.0 1.5 %collective-permute-start.4 = (f32[2,4,16,128]{3,2,1,0:T(8,128)S(1)}, f32[2,4,16,128]{3,2,1,0:T(8,128)S(1)}, u32[]{:S(2)}, u32[]{:S(2)}) collective-permute-start(f32[2,4,16,128]{3,2,1,0:T(8,128)S(1)} %get-tuple-element.11.args_0_), channel_id=1, source_target_pairs={{8,0},{12,4},{0,8},{4,12},{24,16},{28,20},{16,24},{20,28},{9,1},{1... | collective-permute-start | bytes 196616 | tf_op jit(solution)/shard_map/ppermute | solution.py:245
  26.5 1.7 %collective-permute-done.6.args_3_ = f32[2,4,16,128]{3,2,1,0:T(8,128)S(1)} collective-permute-done((f32[2,4,16,128]{3,2,1,0:T(8,128)S(1)}, f32[2,4,16,128]{3,2,1,0:T(8,128)S(1)}, u32[]{:S(2)}, u32[]{:S(2)}) %collective-permute-start.6) | collective-permute-done | bytes 65568 | tf_op jit(solution)/shard_map/ppermute | solution.py:245
  28.3 0.6 %collective-permute-done.5.args_2_ = f32[2,4,16,128]{3,2,1,0:T(8,128)S(1)} collective-permute-done((f32[2,4,16,128]{3,2,1,0:T(8,128)S(1)}, f32[2,4,16,128]{3,2,1,0:T(8,128)S(1)}, u32[]{:S(2)}, u32[]{:S(2)}) %collective-permute-start.5) | collective-permute-done | bytes 65568 | tf_op jit(solution)/shard_map/ppermute | solution.py:245
  28.9 0.4 %collective-permute-done.4.args_1_ = f32[2,4,16,128]{3,2,1,0:T(8,128)S(1)} collective-permute-done((f32[2,4,16,128]{3,2,1,0:T(8,128)S(1)}, f32[2,4,16,128]{3,2,1,0:T(8,128)S(1)}, u32[]{:S(2)}, u32[]{:S(2)}) %collective-permute-start.4) | collective-permute-done | bytes 65568 | tf_op jit(solution)/shard_map/ppermute | solution.py:245
  29.3 0.7 %assemble.1 = (f32[4,64,128]{2,1,0:T(8,128)}, f32[4,64,128]{2,1,0:T(8,128)}, f32[4,128]{1,0:T(4,128)}) custom-call(f32[2,4,16,128]{3,2,1,0:T(8,128)S(1)} %get-tuple-element.11.args_0_, f32[2,4,16,128]{3,2,1,0:T(8,128)S(1)} %collective-permute-done.4.args_1_, f32[2,4,16,128]{3,2,1,0:T(8,128)S(1)} %collective-permute-done.5.args_2_, ...), custom_call_target="tpu_custom_call" | custom-call | tf_op jit(solution)/shard_map/assemble/pallas_call | solution.py:380
  (2 shorter events, 0.0 us)
Async XLA Ops:
  1.4 4.8 %copy-start = (bf16[1024,1024]{1,0:T(8,128)(2,1)S(1)}, bf16[1024,1024]{1,0:T(8,128)(2,1)}, u32[]{:S(2)}) copy-start(bf16[1024,1024]{1,0:T(8,128)(2,1)} %args_5_.4) | copy-start | bytes 6291460
  1.4 4.8 %copy-start.1 = (bf16[256,1024]{1,0:T(8,128)(2,1)S(1)}, bf16[256,1024]{1,0:T(8,128)(2,1)}, u32[]{:S(2)}) copy-start(bf16[256,1024]{1,0:T(8,128)(2,1)} %args_4_.6) | copy-start | bytes 1572868
  1.4 4.8 %copy-start.2 = (bf16[1024,128]{1,0:T(8,128)(2,1)S(1)}, bf16[1024,128]{1,0:T(8,128)(2,1)}, u32[]{:S(2)}) copy-start(bf16[1024,128]{1,0:T(8,128)(2,1)} %args_6_.4) | copy-start | bytes 786436
  1.4 4.8 %copy-start.3 = (f32[256]{0:T(256)S(1)}, f32[256]{0:T(256)}, u32[]{:S(2)}) copy-start(f32[256]{0:T(256)} %param.10) | copy-start | bytes 3076
  1.4 4.8 %copy-start.4 = (s32[64]{0:T(128)S(1)}, s32[64]{0:T(128)}, u32[]{:S(2)}) copy-start(s32[64]{0:T(128)} %param.14) | copy-start | bytes 772
  1.4 4.8 %copy-start.5 = (s32[4]{0:T(128)S(1)}, s32[4]{0:T(128)}, u32[]{:S(2)}) copy-start(s32[4]{0:T(128)} %param.15) | copy-start | bytes 52
  1.4 7.2 %collective-permute-start.2 = (f32[2,4,8,256]{3,2,1,0:T(8,128)S(1)}, f32[2,4,8,256]{3,2,1,0:T(8,128)S(1)}, u32[]{:S(2)}, u32[]{:S(2)}) collective-permute-start(f32[2,4,8,256]{3,2,1,0:T(8,128)S(1)} %pass.1.args_0_), channel_id=1, source_target_pairs={{12,0},{8,4},{4,8},{0,12},{28,16},{24,20},{20,24},{16,28},{13,1},{... | collective-permute-start | bytes 196616 | tf_op jit(solution)/shard_map/ppermute | solution.py:245
  5.5 4.3 %collective-permute-start.1 = (f32[2,4,8,256]{3,2,1,0:T(8,128)S(1)}, f32[2,4,8,256]{3,2,1,0:T(8,128)S(1)}, u32[]{:S(2)}, u32[]{:S(2)}) collective-permute-start(f32[2,4,8,256]{3,2,1,0:T(8,128)S(1)} %pass.1.args_0_), channel_id=1, source_target_pairs={{4,0},{0,4},{12,8},{8,12},{20,16},{16,20},{28,24},{24,28},{5,1},{1... | collective-permute-start | bytes 196616 | tf_op jit(solution)/shard_map/ppermute | solution.py:245
  6.0 4.3 %collective-permute-start = (f32[2,4,8,256]{3,2,1,0:T(8,128)S(1)}, f32[2,4,8,256]{3,2,1,0:T(8,128)S(1)}, u32[]{:S(2)}, u32[]{:S(2)}) collective-permute-start(f32[2,4,8,256]{3,2,1,0:T(8,128)S(1)} %pass.1.args_0_), channel_id=1, source_target_pairs={{8,0},{12,4},{0,8},{4,12},{24,16},{28,20},{16,24},{20,28},{9,1},{1... | collective-permute-start | bytes 196616 | tf_op jit(solution)/shard_map/ppermute | solution.py:245
  16.2 6.7 %collective-permute-start.3 = (f32[208,128]{1,0:T(8,128)S(1)}, f32[208,128]{1,0:T(8,128)S(1)}, u32[]{:S(2)}, u32[]{:S(2)}) collective-permute-start(f32[208,128]{1,0:T(8,128)S(1)} %late.1.own_ref), channel_id=1, source_target_pairs={{0,16},{4,20},{8,24},{12,28},{16,0},{20,4},{24,8},{28,12},{1,17},{... | collective-permute-start | bytes 319496 | tf_op jit(solution)/shard_map/ppermute | solution.py:245
  23.0 5.3 %collective-permute-start.6 = (f32[2,4,16,128]{3,2,1,0:T(8,128)S(1)}, f32[2,4,16,128]{3,2,1,0:T(8,128)S(1)}, u32[]{:S(2)}, u32[]{:S(2)}) collective-permute-start(f32[2,4,16,128]{3,2,1,0:T(8,128)S(1)} %get-tuple-element.11.args_0_), channel_id=1, source_target_pairs={{12,0},{8,4},{4,8},{0,12},{28,16},{24,20},{20,24},{16,28},{13,1},{... | collective-permute-start | bytes 196616 | tf_op jit(solution)/shard_map/ppermute | solution.py:245
  23.9 5.0 %collective-permute-start.5 = (f32[2,4,16,128]{3,2,1,0:T(8,128)S(1)}, f32[2,4,16,128]{3,2,1,0:T(8,128)S(1)}, u32[]{:S(2)}, u32[]{:S(2)}) collective-permute-start(f32[2,4,16,128]{3,2,1,0:T(8,128)S(1)} %get-tuple-element.11.args_0_), channel_id=1, source_target_pairs={{4,0},{0,4},{12,8},{8,12},{20,16},{16,20},{28,24},{24,28},{5,1},{1... | collective-permute-start | bytes 196616 | tf_op jit(solution)/shard_map/ppermute | solution.py:245
  25.0 4.3 %collective-permute-start.4 = (f32[2,4,16,128]{3,2,1,0:T(8,128)S(1)}, f32[2,4,16,128]{3,2,1,0:T(8,128)S(1)}, u32[]{:S(2)}, u32[]{:S(2)}) collective-permute-start(f32[2,4,16,128]{3,2,1,0:T(8,128)S(1)} %get-tuple-element.11.args_0_), channel_id=1, source_target_pairs={{8,0},{12,4},{0,8},{4,12},{24,16},{28,20},{16,24},{20,28},{9,1},{1... | collective-permute-start | bytes 196616 | tf_op jit(solution)/shard_map/ppermute | solution.py:245

commit v5 on v4

--- a/solution.py
+++ b/solution.py
@@ -200,7 +200,8 @@
         slot = index % 2
         if index + 1 < len(chunks):
             fill(chunks[index + 1], rows, pre_ref, delta, picked, first_ref.at[1 - slot])
-        result_ref[slot] = tail(first_ref.at[slot], second_ref.at[slot], two_ref, three_ref)
+        held = pl.ds(0, len(units) * rows)
+        result_ref[slot, held] = tail(first_ref.at[slot, held], second_ref.at[slot, held], two_ref, three_ref)
         tally(units, front - 1, windows, block_rows, mask_of, result_ref.at[slot], base_ref, base_sums, store)
 
 
@@ -256,7 +257,7 @@
     groups = total_groups // front
     late_rows = (front - 1) * windows * block_rows
     per_chunk = units_per_chunk(groups + 2, late_rows)
-    chunks = [range(at, at + per_chunk) for at in range(0, groups + 2, per_chunk)]
+    chunks = [range(at, min(at + per_chunk + 1, groups + 2)) for at in range(0, groups + 2, per_chunk + 1)]
     height = (3 * groups + 4) * windows
     order = order_of(front)
 
@@ -335,7 +336,7 @@
     def late(*args):
         return late_kernel(front, chunks, *args)
 
-    chunk_rows = per_chunk * late_rows
+    chunk_rows = len(chunks[0]) * late_rows
     late_scratch = [
         pltpu.VMEM((2 * late_rows, hidden), jnp.float32),
         pltpu.VMEM((2, chunk_rows, hidden), jnp.bfloat16),

time: 30.3 us -> 30.3 us (level)
  no operation moved by 1% of the time
where the time goes in v5:
time: 30.3 us; the launch traced here: 30 us
  starting transfers between devices  10.9 us (36%)
  Pallas kernels  9.09 us (30%)
  waiting for transfers between devices  8.48 us (28%)
  other arithmetic  0.74 us (2%)
  between operations  0.73 us (2%)
    ppermute x7, starting transfers between devices, exchange(): return lax.ppermute(values, 'rows', pairs)  10.9 us
    ppermute x7, waiting for transfers between devices, exchange(): return lax.ppermute(values, 'rows', pairs)  8.48 us
    pallas_call x1, Pallas kernels, local(): pl.pallas_call(late, out_shape=pltpu.VMEM((height, outputs), jnp.float32)...  5.92 us
    pallas_call x1, Pallas kernels, local(): pl.pallas_call(early, out_shape=(pltpu.VMEM((height, outputs), jnp.float3...  2.42 us
    convert_element_type x1, other arithmetic, local(): own = jnp.stack([base_a, base_b]).astype(jnp.float32)  0.74 us
    pallas_call x1, Pallas kernels, local(): pl.pallas_call(assemble, out_shape=(whole, whole, jax.ShapeDtypeStruct((w...  0.72 us
  transfers between devices with their start and end apart: 7, of which 6 were waited for; matrix products, arithmetic and copies ran while one was open for 0% of the time, Pallas kernels for 8%

profile of v5, /device:TPU:0, one launch (start us, length us, event | category | flops | bytes accessed | tf_op | source)
XLA Modules:
  0.0 30.0 jit_solution(12656632237298421994)
XLA Ops:
  0.6 0.7 %maximum_convert_fusion.given_ref = f32[2,4,8,256]{3,2,1,0:T(8,128)S(1)} fusion(bf16[1,4,8,256]{3,2,1,0:T(8,128)(2,1)} %bitcast.9, bf16[1,4,8,256]{3,2,1,0:T(8,128)(2,1)} %bitcast.10), kind=kLoop, calls=%fused_computation | loop fusion | flops 32768 | bytes 98304 | tf_op jit(solution)/shard_map/convert_element_type | solution.py:285
  1.4 0.0 copy-start
  1.4 0.0 copy-start.1
  1.4 0.0 copy-start.2
  1.4 0.0 copy-start.3
  1.4 0.0 copy-start.4
  1.4 0.0 copy-start.5
  1.4 4.1 %collective-permute-start.2 = (f32[2,4,8,256]{3,2,1,0:T(8,128)S(1)}, f32[2,4,8,256]{3,2,1,0:T(8,128)S(1)}, u32[]{:S(2)}, u32[]{:S(2)}) collective-permute-start(f32[2,4,8,256]{3,2,1,0:T(8,128)S(1)} %pass.1.args_0_), channel_id=1, source_target_pairs={{12,0},{8,4},{4,8},{0,12},{28,16},{24,20},{20,24},{16,28},{13,1},{... | collective-permute-start | bytes 196616 | tf_op jit(solution)/shard_map/ppermute | solution.py:246
  5.5 0.5 %collective-permute-start.1 = (f32[2,4,8,256]{3,2,1,0:T(8,128)S(1)}, f32[2,4,8,256]{3,2,1,0:T(8,128)S(1)}, u32[]{:S(2)}, u32[]{:S(2)}) collective-permute-start(f32[2,4,8,256]{3,2,1,0:T(8,128)S(1)} %pass.1.args_0_), channel_id=1, source_target_pairs={{4,0},{0,4},{12,8},{8,12},{20,16},{16,20},{28,24},{24,28},{5,1},{1... | collective-permute-start | bytes 196616 | tf_op jit(solution)/shard_map/ppermute | solution.py:246
  6.0 0.1 collective-permute-start
  6.2 0.0 copy-done
  6.2 0.0 copy-done.1
  6.2 0.0 copy-done.2
  6.2 0.0 copy-done.3
  6.2 0.0 copy-done.4
  6.2 0.0 copy-done.5
  6.2 2.4 %early.1 = (f32[208,128]{1,0:T(8,128)S(1)}, bf16[16,256]{1,0:T(8,128)(2,1)S(1)}, f32[4,4,8,128]{3,2,1,0:T(8,128)S(1)}) custom-call(f32[2,4,8,256]{3,2,1,0:T(8,128)S(1)} %pass.1.args_0_, f32[1,256]{1,0:T(1,128)S(1)} %bitcast.5, bf16[256,1024]{1,0:T(8,128)(2,1)S(1)} %copy-done.1, bf16[1024,1024]{1,0:T(8,128)(2,1)S(1)} %copy-done, ...), custom_call_target="tpu_custom_call" | custom-call | flops 1358954496 | bytes 2883584 | tf_op jit(solution)/shard_map/early/pallas_call | solution.py:313
  8.6 0.0 collective-permute-done.2.args_2_
  8.6 1.2 %collective-permute-done.1.args_1_ = f32[2,4,8,256]{3,2,1,0:T(8,128)S(1)} collective-permute-done((f32[2,4,8,256]{3,2,1,0:T(8,128)S(1)}, f32[2,4,8,256]{3,2,1,0:T(8,128)S(1)}, u32[]{:S(2)}, u32[]{:S(2)}) %collective-permute-start.1) | collective-permute-done | bytes 65568 | tf_op jit(solution)/shard_map/ppermute | solution.py:246
  9.8 0.5 %collective-permute-done.args_0_ = f32[2,4,8,256]{3,2,1,0:T(8,128)S(1)} collective-permute-done((f32[2,4,8,256]{3,2,1,0:T(8,128)S(1)}, f32[2,4,8,256]{3,2,1,0:T(8,128)S(1)}, u32[]{:S(2)}, u32[]{:S(2)}) %collective-permute-start) | collective-permute-done | bytes 65568 | tf_op jit(solution)/shard_map/ppermute | solution.py:246
  10.3 5.9 %late.1.own_ref = f32[208,128]{1,0:T(8,128)S(1)} custom-call(f32[2,4,8,256]{3,2,1,0:T(8,128)S(1)} %collective-permute-done.args_0_, f32[2,4,8,256]{3,2,1,0:T(8,128)S(1)} %collective-permute-done.1.args_1_, f32[2,4,8,256]{3,2,1,0:T(8,128)S(1)} %collective-permute-done.2.args_2_, f32[1,256]{1,0:T(1,128)S(1)} %bitcast.6, bf16[256,1024]{1,0:T(8,128)(2,1)S(1)} %copy-done.1, ...), custom_call_target="tpu_custom_call" | custom-call | flops 4756340736 | bytes 2883584 | tf_op jit(solution)/shard_map/late/pallas_call | solution.py:347
  16.2 2.7 %collective-permute-start.3 = (f32[208,128]{1,0:T(8,128)S(1)}, f32[208,128]{1,0:T(8,128)S(1)}, u32[]{:S(2)}, u32[]{:S(2)}) collective-permute-start(f32[208,128]{1,0:T(8,128)S(1)} %late.1.own_ref), channel_id=1, source_target_pairs={{0,16},{4,20},{8,24},{12,28},{16,0},{20,4},{24,8},{28,12},{1,17},{... | collective-permute-start | bytes 319496 | tf_op jit(solution)/shard_map/ppermute | solution.py:246
  18.9 4.1 %collective-permute-done.3.other_ref = f32[208,128]{1,0:T(8,128)S(1)} collective-permute-done((f32[208,128]{1,0:T(8,128)S(1)}, f32[208,128]{1,0:T(8,128)S(1)}, u32[]{:S(2)}, u32[]{:S(2)}) %collective-permute-start.3) | collective-permute-done | bytes 106528 | tf_op jit(solution)/shard_map/ppermute | solution.py:246
  23.0 1.0 %collective-permute-start.6 = (f32[2,4,16,128]{3,2,1,0:T(8,128)S(1)}, f32[2,4,16,128]{3,2,1,0:T(8,128)S(1)}, u32[]{:S(2)}, u32[]{:S(2)}) collective-permute-start(f32[2,4,16,128]{3,2,1,0:T(8,128)S(1)} %get-tuple-element.11.args_0_), channel_id=1, source_target_pairs={{12,0},{8,4},{4,8},{0,12},{28,16},{24,20},{20,24},{16,28},{13,1},{... | collective-permute-start | bytes 196616 | tf_op jit(solution)/shard_map/ppermute | solution.py:246
  23.9 1.1 %collective-permute-start.5 = (f32[2,4,16,128]{3,2,1,0:T(8,128)S(1)}, f32[2,4,16,128]{3,2,1,0:T(8,128)S(1)}, u32[]{:S(2)}, u32[]{:S(2)}) collective-permute-start(f32[2,4,16,128]{3,2,1,0:T(8,128)S(1)} %get-tuple-element.11.args_0_), channel_id=1, source_target_pairs={{4,0},{0,4},{12,8},{8,12},{20,16},{16,20},{28,24},{24,28},{5,1},{1... | collective-permute-start | bytes 196616 | tf_op jit(solution)/shard_map/ppermute | solution.py:246
  25.0 1.5 %collective-permute-start.4 = (f32[2,4,16,128]{3,2,1,0:T(8,128)S(1)}, f32[2,4,16,128]{3,2,1,0:T(8,128)S(1)}, u32[]{:S(2)}, u32[]{:S(2)}) collective-permute-start(f32[2,4,16,128]{3,2,1,0:T(8,128)S(1)} %get-tuple-element.11.args_0_), channel_id=1, source_target_pairs={{8,0},{12,4},{0,8},{4,12},{24,16},{28,20},{16,24},{20,28},{9,1},{1... | collective-permute-start | bytes 196616 | tf_op jit(solution)/shard_map/ppermute | solution.py:246
  26.5 1.7 %collective-permute-done.6.args_3_ = f32[2,4,16,128]{3,2,1,0:T(8,128)S(1)} collective-permute-done((f32[2,4,16,128]{3,2,1,0:T(8,128)S(1)}, f32[2,4,16,128]{3,2,1,0:T(8,128)S(1)}, u32[]{:S(2)}, u32[]{:S(2)}) %collective-permute-start.6) | collective-permute-done | bytes 65568 | tf_op jit(solution)/shard_map/ppermute | solution.py:246
  28.3 0.6 %collective-permute-done.5.args_2_ = f32[2,4,16,128]{3,2,1,0:T(8,128)S(1)} collective-permute-done((f32[2,4,16,128]{3,2,1,0:T(8,128)S(1)}, f32[2,4,16,128]{3,2,1,0:T(8,128)S(1)}, u32[]{:S(2)}, u32[]{:S(2)}) %collective-permute-start.5) | collective-permute-done | bytes 65568 | tf_op jit(solution)/shard_map/ppermute | solution.py:246
  28.9 0.4 %collective-permute-done.4.args_1_ = f32[2,4,16,128]{3,2,1,0:T(8,128)S(1)} collective-permute-done((f32[2,4,16,128]{3,2,1,0:T(8,128)S(1)}, f32[2,4,16,128]{3,2,1,0:T(8,128)S(1)}, u32[]{:S(2)}, u32[]{:S(2)}) %collective-permute-start.4) | collective-permute-done | bytes 65568 | tf_op jit(solution)/shard_map/ppermute | solution.py:246
  29.3 0.7 %assemble.1 = (f32[4,64,128]{2,1,0:T(8,128)}, f32[4,64,128]{2,1,0:T(8,128)}, f32[4,128]{1,0:T(4,128)}) custom-call(f32[2,4,16,128]{3,2,1,0:T(8,128)S(1)} %get-tuple-element.11.args_0_, f32[2,4,16,128]{3,2,1,0:T(8,128)S(1)} %collective-permute-done.4.args_1_, f32[2,4,16,128]{3,2,1,0:T(8,128)S(1)} %collective-permute-done.5.args_2_, ...), custom_call_target="tpu_custom_call" | custom-call | tf_op jit(solution)/shard_map/assemble/pallas_call | solution.py:381
  (2 shorter events, 0.0 us)
Async XLA Ops:
  1.4 4.8 %copy-start = (bf16[1024,1024]{1,0:T(8,128)(2,1)S(1)}, bf16[1024,1024]{1,0:T(8,128)(2,1)}, u32[]{:S(2)}) copy-start(bf16[1024,1024]{1,0:T(8,128)(2,1)} %args_5_.4) | copy-start | bytes 6291460
  1.4 4.8 %copy-start.1 = (bf16[256,1024]{1,0:T(8,128)(2,1)S(1)}, bf16[256,1024]{1,0:T(8,128)(2,1)}, u32[]{:S(2)}) copy-start(bf16[256,1024]{1,0:T(8,128)(2,1)} %args_4_.6) | copy-start | bytes 1572868
  1.4 4.8 %copy-start.2 = (bf16[1024,128]{1,0:T(8,128)(2,1)S(1)}, bf16[1024,128]{1,0:T(8,128)(2,1)}, u32[]{:S(2)}) copy-start(bf16[1024,128]{1,0:T(8,128)(2,1)} %args_6_.4) | copy-start | bytes 786436
  1.4 4.8 %copy-start.3 = (f32[256]{0:T(256)S(1)}, f32[256]{0:T(256)}, u32[]{:S(2)}) copy-start(f32[256]{0:T(256)} %param.10) | copy-start | bytes 3076
  1.4 4.8 %copy-start.4 = (s32[64]{0:T(128)S(1)}, s32[64]{0:T(128)}, u32[]{:S(2)}) copy-start(s32[64]{0:T(128)} %param.14) | copy-start | bytes 772
  1.4 4.8 %copy-start.5 = (s32[4]{0:T(128)S(1)}, s32[4]{0:T(128)}, u32[]{:S(2)}) copy-start(s32[4]{0:T(128)} %param.15) | copy-start | bytes 52
  1.4 7.2 %collective-permute-start.2 = (f32[2,4,8,256]{3,2,1,0:T(8,128)S(1)}, f32[2,4,8,256]{3,2,1,0:T(8,128)S(1)}, u32[]{:S(2)}, u32[]{:S(2)}) collective-permute-start(f32[2,4,8,256]{3,2,1,0:T(8,128)S(1)} %pass.1.args_0_), channel_id=1, source_target_pairs={{12,0},{8,4},{4,8},{0,12},{28,16},{24,20},{20,24},{16,28},{13,1},{... | collective-permute-start | bytes 196616 | tf_op jit(solution)/shard_map/ppermute | solution.py:246
  5.5 4.3 %collective-permute-start.1 = (f32[2,4,8,256]{3,2,1,0:T(8,128)S(1)}, f32[2,4,8,256]{3,2,1,0:T(8,128)S(1)}, u32[]{:S(2)}, u32[]{:S(2)}) collective-permute-start(f32[2,4,8,256]{3,2,1,0:T(8,128)S(1)} %pass.1.args_0_), channel_id=1, source_target_pairs={{4,0},{0,4},{12,8},{8,12},{20,16},{16,20},{28,24},{24,28},{5,1},{1... | collective-permute-start | bytes 196616 | tf_op jit(solution)/shard_map/ppermute | solution.py:246
  6.0 4.3 %collective-permute-start = (f32[2,4,8,256]{3,2,1,0:T(8,128)S(1)}, f32[2,4,8,256]{3,2,1,0:T(8,128)S(1)}, u32[]{:S(2)}, u32[]{:S(2)}) collective-permute-start(f32[2,4,8,256]{3,2,1,0:T(8,128)S(1)} %pass.1.args_0_), channel_id=1, source_target_pairs={{8,0},{12,4},{0,8},{4,12},{24,16},{28,20},{16,24},{20,28},{9,1},{1... | collective-permute-start | bytes 196616 | tf_op jit(solution)/shard_map/ppermute | solution.py:246
  16.2 6.7 %collective-permute-start.3 = (f32[208,128]{1,0:T(8,128)S(1)}, f32[208,128]{1,0:T(8,128)S(1)}, u32[]{:S(2)}, u32[]{:S(2)}) collective-permute-start(f32[208,128]{1,0:T(8,128)S(1)} %late.1.own_ref), channel_id=1, source_target_pairs={{0,16},{4,20},{8,24},{12,28},{16,0},{20,4},{24,8},{28,12},{1,17},{... | collective-permute-start | bytes 319496 | tf_op jit(solution)/shard_map/ppermute | solution.py:246
  23.0 5.3 %collective-permute-start.6 = (f32[2,4,16,128]{3,2,1,0:T(8,128)S(1)}, f32[2,4,16,128]{3,2,1,0:T(8,128)S(1)}, u32[]{:S(2)}, u32[]{:S(2)}) collective-permute-start(f32[2,4,16,128]{3,2,1,0:T(8,128)S(1)} %get-tuple-element.11.args_0_), channel_id=1, source_target_pairs={{12,0},{8,4},{4,8},{0,12},{28,16},{24,20},{20,24},{16,28},{13,1},{... | collective-permute-start | bytes 196616 | tf_op jit(solution)/shard_map/ppermute | solution.py:246
  23.9 5.0 %collective-permute-start.5 = (f32[2,4,16,128]{3,2,1,0:T(8,128)S(1)}, f32[2,4,16,128]{3,2,1,0:T(8,128)S(1)}, u32[]{:S(2)}, u32[]{:S(2)}) collective-permute-start(f32[2,4,16,128]{3,2,1,0:T(8,128)S(1)} %get-tuple-element.11.args_0_), channel_id=1, source_target_pairs={{4,0},{0,4},{12,8},{8,12},{20,16},{16,20},{28,24},{24,28},{5,1},{1... | collective-permute-start | bytes 196616 | tf_op jit(solution)/shard_map/ppermute | solution.py:246
  25.0 4.3 %collective-permute-start.4 = (f32[2,4,16,128]{3,2,1,0:T(8,128)S(1)}, f32[2,4,16,128]{3,2,1,0:T(8,128)S(1)}, u32[]{:S(2)}, u32[]{:S(2)}) collective-permute-start(f32[2,4,16,128]{3,2,1,0:T(8,128)S(1)} %get-tuple-element.11.args_0_), channel_id=1, source_target_pairs={{8,0},{12,4},{0,8},{4,12},{24,16},{28,20},{16,24},{20,28},{9,1},{1... | collective-permute-start | bytes 196616 | tf_op jit(solution)/shard_map/ppermute | solution.py:246
